TPU v7x, 32 devices: a whole 2x2x4 slice. The times are simulated.
32 devices in a mesh: head: 4 (over z), outer: 2 (over core), inner: 4 (over y, x).
Axes of the slice: x: 2, y: 2, z: 4, core: 2. Of those that a mesh axis runs over, the one named last changes fastest.
Arguments:
- query: bfloat16 [2048, 64, 128], P(('outer', 'inner'), 'head'), may hold values from -24 to 24
- keys: bfloat16 [2048, 8, 128], P(('outer', 'inner'), 'head'), may hold values from -8 to 8
- values: bfloat16 [2048, 8, 128], P(('outer', 'inner'), 'head'), may hold values from -6 to 6
- forward_output: bfloat16 [2048, 64, 128], P(('outer', 'inner'), 'head'), may hold values from -2.390625 to 2.390625
- d_out: bfloat16 [2048, 64, 128], P(('outer', 'inner'), 'head'), may hold values from -2.390625 to 2.390625
- span_order: int32 [1, 8], replicated, may hold values from 0 to 7, each once within a row
Outputs:
- d_query: bfloat16 [8, 256, 64, 128], P(('outer', 'inner'), 'head')
- key_gradient: bfloat16 [8, 256, 8, 128], P(('outer', 'inner'), 'head')
- value_gradient: bfloat16 [8, 256, 8, 128], P(('outer', 'inner'), 'head')
Inputs may be any that keep to these rules, and one draw needn't show every extreme that they name: `span_order`: each row holds every number once.
All inputs are finite; a program needn't handle non-finite values.
Results may differ from a plain program's by a relative error of at most 0.0051.
Values may be sent and summed in bfloat16 or wider, within the bound.
No kernel may reach another device: no remote copies, remote signals or barrier semaphores. Data moves between devices by JAX's collectives and lax.ppermute only.
A program may use at most 64 MiB of HBM per device.

v0:
```python
import functools
import math

import jax
import jax.numpy as jnp
from jax import lax
from jax.experimental import pallas as pl
from jax.experimental.pallas import tpu as pltpu
from jax.sharding import PartitionSpec as P


F32 = jnp.float32
BF16 = jnp.bfloat16
NT = (((1,), (1,)), ((), ()))
NN = (((1,), (0,)), ((), ()))
MASKED = -1e30
VMEM = pl.BlockSpec(memory_space=pltpu.VMEM)
SMEM = pl.BlockSpec(memory_space=pltpu.SMEM)


def dot(a, b, dims):
    return lax.dot_general(a, b, dims, preferred_element_type=F32)


def causal_tile(rows):
    shape = (rows, rows)
    return lax.broadcasted_iota(jnp.int32, shape, 0) <= lax.broadcasted_iota(jnp.int32, shape, 1)


def over_visible(place, tile):
    tile(place, True)

    def turn(k, _):
        tile(k, False)
        return 0

    lax.fori_loop(0, place, turn, 0)


def lse_kernel(group, scale, blocks, table, *refs):
    slots = (len(refs) - 3) // 2
    q_refs, kv_ref, lse_refs = refs[:slots], refs[slots], refs[slots + 1 : 2 * slots + 1]
    m_ref, l_ref = refs[-2:]
    heads, rows, _ = q_refs[0].shape
    scale2 = scale * math.log2(math.e)
    causal = causal_tile(rows)
    for q_ref, lse_ref, s in zip(q_refs, lse_refs, range(slots)):
        for g in range(0, heads, group):

            def tile(k, diag):
                keys = kv_ref[table[k], 0]
                for j in range(g, g + group):
                    st = dot(keys, q_ref[j], NT)
                    if diag:
                        st = jnp.where(causal, st, MASKED)
                    st = st.reshape(rows // 8, 8, rows)
                    m_new = jnp.max(st, axis=0)
                    if not diag:
                        m_old = m_ref[j - g]
                        m_new = jnp.maximum(m_old, m_new)
                    total = jnp.sum(jnp.exp2((st - m_new[None]) * scale2), axis=0)
                    if not diag:
                        total = total + l_ref[j - g] * jnp.exp2((m_old - m_new) * scale2)
                    m_ref[j - g] = m_new
                    l_ref[j - g] = total

            over_visible(table[blocks + s], tile)
            for j in range(g, g + group):
                m = m_ref[j - g]
                high = jnp.max(m, axis=0, keepdims=True)
                total = jnp.sum(
                    l_ref[j - g] * jnp.exp2((m - high) * scale2), axis=0, keepdims=True
                )
                lse_ref[j : j + 1, :] = high * scale2 + jnp.log2(total)


def lse_call(table, q, kv, group, scale):
    heads, rows, width = q[0].shape
    blocks = kv.shape[0]
    flops = len(q) * heads * rows * rows * blocks * width
    return pl.pallas_call(
        functools.partial(lse_kernel, group, scale, blocks),
        out_shape=[jax.ShapeDtypeStruct((heads, rows), F32)] * len(q),
        in_specs=[SMEM] + [VMEM] * (len(q) + 1),
        out_specs=[VMEM] * len(q),
        scratch_shapes=[pltpu.VMEM((group, 8, rows), F32)] * 2,
        cost_estimate=pl.CostEstimate(flops=flops, bytes_accessed=q[0].size * 4, transcendentals=0),
        name="lse",
    )(table, *q, kv)


def grad_kernel(group, scale, inner, slots, table, *refs):
    q_refs, do_refs, lse_refs, delta_refs = (refs[k * slots : (k + 1) * slots] for k in range(4))
    kv_ref, dq_ref = refs[4 * slots], refs[4 * slots + 1]
    out_refs = refs[4 * slots + 2 : 4 * slots + 2 + inner]
    kt_ref, dqt_ref, dka_ref, dva_ref = refs[-4:]
    heads, rows, _ = q_refs[0].shape
    blocks = kv_ref.shape[0]
    slice_rows = dq_ref.shape[2]
    zs = rows // slice_rows
    scale2 = scale * math.log2(math.e)
    causal = causal_tile(rows)
    core, place_in, z_in = (table[blocks + slots + k] for k in range(3))
    dka_ref[...] = jnp.zeros_like(dka_ref)
    dva_ref[...] = jnp.zeros_like(dva_ref)
    for b in range(blocks):
        kt_ref[b] = kv_ref[b, 0].T
    for s in range(slots):
        q_ref, do_ref, lse_ref, delta_ref = q_refs[s], do_refs[s], lse_refs[s], delta_refs[s]
        for g in range(0, heads, group):

            def tile(k, diag):
                block = table[k]
                keys, vals, keys_t = kv_ref[block, 0], kv_ref[block, 1], kt_ref[block]
                dk, dv = dka_ref[block], dva_ref[block]
                for j in range(g, g + group):
                    st = dot(keys, q_ref[j], NT)
                    dp = dot(vals, do_ref[j], NT)
                    p = jnp.exp2(st * scale2 - lse_ref[j : j + 1, :])
                    if diag:
                        p = jnp.where(causal, p, 0.0)
                    ds = (p * (dp - delta_ref[j : j + 1, :])).astype(BF16)
                    dv = dv + dot(p.astype(BF16), do_ref[j], NN)
                    dk = dk + dot(ds, q_ref[j], NN)
                    part = dot(keys_t, ds, NN)
                    if diag:
                        dqt_ref[j - g] = part
                    else:
                        dqt_ref[j - g] += part
                dka_ref[block] = dk
                dva_ref[block] = dv

            over_visible(table[blocks + s], tile)
            to_core = lax.rem(core + s, slots)
            for j in range(g, g + group):
                dq = (dqt_ref[j - g] * scale).T.astype(BF16)
                for z in range(zs):
                    dq_ref[to_core * zs + z, j] = dq[z * slice_rows : (z + 1) * slice_rows]
    for step, out_ref in enumerate(out_refs):
        for c in range(slots):
            block = partner(core, c, slots) * inner + partner(place_in, step, inner)
            for z in range(zs):
                start = pl.multiple_of(partner(z_in, z, zs) * slice_rows, slice_rows)
                cut = pl.ds(start, slice_rows)
                out_ref[c * zs + z, 0] = (dka_ref[block, cut] * scale).astype(BF16)
                out_ref[c * zs + z, 1] = dva_ref[block, cut].astype(BF16)


def grad_call(table, q, do, lse, delta, kv, group, scale, inner, zs):
    heads, rows, width = q[0].shape
    slots, blocks = len(q), kv.shape[0]
    slice_rows = rows // zs
    flops = 5 * slots * heads * rows * rows * blocks * width
    outs = [(slots * zs, heads, slice_rows, width)] + [(slots * zs, 2, slice_rows, width)] * inner
    return pl.pallas_call(
        functools.partial(grad_kernel, group, scale, inner, slots),
        out_shape=[jax.ShapeDtypeStruct(shape, BF16) for shape in outs],
        in_specs=[SMEM] + [VMEM] * (4 * slots + 1),
        out_specs=[VMEM] * len(outs),
        scratch_shapes=[
            pltpu.VMEM((blocks, width, rows), BF16),
            pltpu.VMEM((group, width, rows), F32),
            pltpu.VMEM((blocks, rows, width), F32),
            pltpu.VMEM((blocks, rows, width), F32),
        ],
        cost_estimate=pl.CostEstimate(flops=flops, bytes_accessed=q[0].size * 12, transcendentals=0),
        name="grads",
    )(table, *q, *do, *lse, *delta, kv)


def exchange(x, axes):
    return lax.all_to_all(x, axes, split_axis=0, concat_axis=0, tiled=True)


def partner(index, step, count):
    if count & (count - 1) == 0:
        return index ^ step
    return (step - index) % count


def trade(x, axis, step):
    count = lax.axis_size(axis)
    return lax.ppermute(x, axis, [(d, partner(d, step, count)) for d in range(count)])


def natural(pieces, index):
    count = len(pieces)

    def pick(place):
        kept = pieces[0]
        for step in range(1, count):
            kept = jnp.where(partner(index, step, count) == place, pieces[step], kept)
        return kept

    return [pick(place) for place in range(count)]


def body(query, keys, values, forward_output, d_out, span_order):
    rows, heads, width = query.shape
    kv_count = keys.shape[1]
    scale = width ** (-0.5)
    cores, inner, zs = lax.axis_size("outer"), lax.axis_size("inner"), lax.axis_size("head")
    core, place, z_in = (lax.axis_index(axis) for axis in ("outer", "inner", "head"))
    blocks = cores * inner
    own_heads = heads // cores
    shared = kv_count % cores != 0
    own_kv = 1 if shared else kv_count // cores
    group_heads = own_heads // own_kv
    slice_rows = rows // zs
    group = min(8, group_heads)

    kv = jnp.stack([jnp.moveaxis(keys, 1, 0), jnp.moveaxis(values, 1, 0)], axis=1)
    kv = jnp.broadcast_to(kv, (cores,) + kv.shape) if shared else kv.reshape((cores, own_kv) + kv.shape[1:])
    kv = jnp.broadcast_to(kv[:, None], (cores, inner) + kv.shape[1:])
    kv = exchange(kv.reshape((blocks,) + kv.shape[2:]), ("outer", "inner"))

    def share(x):
        x = jnp.moveaxis(x, 1, 0)
        x = x.reshape((cores, own_heads) + x.shape[1:])
        got = [lax.dynamic_index_in_dim(x, core, 0, keepdims=False)]
        for step in range(1, cores):
            out = lax.dynamic_index_in_dim(x, (core + step) % cores, 0, keepdims=False)
            got.append(lax.ppermute(out, "outer", [(d, (d + step) % cores) for d in range(cores)]))
        return [got[0]] + got[:0:-1]

    delta = jnp.sum(d_out.astype(F32) * forward_output.astype(F32), axis=-1)
    q_all, do_all, delta_all = share(query), share(d_out), share(delta)

    order = span_order[0]
    ids = jnp.arange(blocks, dtype=jnp.int32)
    by_place = jnp.sum(jnp.where(order[None, :] == ids[:, None], ids[None, :], 0), axis=1)
    own_blocks = (core + jnp.arange(cores, dtype=jnp.int32)) % cores * inner + place
    places = jnp.sum(jnp.where(own_blocks[:, None] == ids[None, :], order[None, :], 0), axis=1)
    table = jnp.concatenate([by_place, places, jnp.stack([core, place, z_in]).astype(jnp.int32)])

    dq, sums = [], []
    for g in range(own_kv):
        q, do, delta_g = (
            [part[g * group_heads : (g + 1) * group_heads] for part in x]
            for x in (q_all, do_all, delta_all)
        )
        lse = lse_call(table, q, kv[:, g], group, scale)
        dq_g, own, *others = grad_call(table, q, do, lse, delta_g, kv[:, g], group, scale, inner, zs)
        dq.append(dq_g)
        total = own.astype(F32)
        for step, part in enumerate(others, 1):
            part = trade(part, "inner", step)
            total = total + part.astype(F32)
        sums.append(total.astype(BF16))

    dq = exchange(jnp.concatenate(dq, axis=1), ("outer", "head"))
    dq = dq.reshape(cores, zs, own_heads, slice_rows, width)
    dq = jnp.transpose(dq, (3, 1, 0, 2, 4)).reshape(1, slice_rows, zs * heads, width)
    sums = jnp.stack(sums, axis=1)
    pieces = [[None] * cores for _ in range(zs)]
    for z in range(zs):
        for c in range(cores):
            pieces[z][c] = sums[c * zs + z]
            if z or c:
                pairs = []
                for d in range(zs * cores):
                    target = partner(d // cores, z, zs) * cores + partner(d % cores, c, cores)
                    pairs.append((d, target))
                pieces[z][c] = lax.ppermute(pieces[z][c], ("head", "outer"), pairs)
    pieces = natural([jnp.stack(natural(row, core)) for row in pieces], z_in)
    sums = jnp.stack(pieces, axis=1)
    if shared:
        sums = jnp.sum(sums.astype(F32), axis=0, keepdims=True).astype(BF16)
    sums = jnp.transpose(sums, (3, 4, 1, 0, 2, 5)).reshape(2, 1, slice_rows, zs * kv_count, width)
    return dq, sums[0], sums[1]


def solution(mesh):
    rows_spec = P(("outer", "inner"), "head", None)
    out_spec = P(("outer", "inner"), "head", None, None)
    return jax.shard_map(
        body,
        mesh=mesh,
        in_specs=(rows_spec,) * 5 + (P(),),
        out_specs=(out_spec,) * 3,
        check_vma=False,
    )
```

profile of v0, /device:TPU:0, one launch (start us, length us, event | category | flops | bytes accessed | tf_op | source)
XLA Modules:
  0.0 104.7 jit_solution(553643606570345614)
XLA Ops:
  0.6 1.4 %pad_maximum_fusion = bf16[2,2,256,128]{3,0,2,1:T(2,128)(2,1)S(1)} fusion(bf16[2,1,256,128]{3,0,2,1:T(2,128)(2,1)} %bitcast.70, bf16[2,1,256,128]{3,0,2,1:T(2,128)(2,1)} %bitcast.71), kind=kLoop, calls=%fused_computation.6 | loop fusion | flops 131072 | bytes 524288 | tf_op jit(solution)/shard_map/stack | solution.py:212
  2.0 1.2 %broadcast_in_dim.39 = bf16[2,4,2,256,128]{4,3,2,1,0:T(8,128)(2,1)} broadcast(bf16[2,2,256,128]{3,2,1,0:T(8,128)(2,1)S(1)} %copy.52), dimensions={0,2,3,4} | broadcast | bytes 1310720 | tf_op jit(solution)/shard_map/broadcast_in_dim | solution.py:214
  3.2 0.0 copy-start
  3.2 0.0 copy-start.1
  3.2 5.3 %all-to-all-start = ((bf16[8,1,2,256,128]{4,3,2,1,0:T(8,128)(2,1)}), bf16[8,1,2,256,128]{4,3,2,1,0:T(8,128)(2,1)}, u32[]{:S(2)}, u32[]{:S(2)}) async-start(bf16[8,1,2,256,128]{4,3,2,1,0:T(8,128)(2,1)} %bitcast.16), calls=%async_computation | async-start | bytes 2097152 | tf_op jit(solution)/shard_map/all_to_all | solution.py:172
  8.5 0.0 copy-done
  8.6 0.0 copy-done.1
  8.6 0.4 constant_dynamic-slice_fusion
  8.9 0.0 copy-start.2
  9.0 0.9 copy.69
  9.8 0.5 collective-permute-start
  10.3 0.9 copy.67
  11.2 0.0 collective-permute-start.1
  11.2 0.0 copy-done.2
  11.2 0.6 multiply_reduce_fusion
  11.8 0.1 copy.53
  11.9 0.6 dynamic-slice_bitcast_fusion
  12.5 0.5 collective-permute-start.2
  13.0 0.0 copy-start.5
  13.0 0.9 copy.70
  13.9 0.9 copy.68
  14.8 0.0 copy-done.5
  14.8 0.1 select_reduce_fusion
  14.9 0.2 fusion
  15.1 0.7 concatenate.147.table
  15.8 0.0 collective-permute-done.refs_1_
  15.8 7.6 %all-to-all-done = bf16[8,1,2,256,128]{4,3,2,1,0:T(8,128)(2,1)} async-done(((bf16[8,1,2,256,128]{4,3,2,1,0:T(8,128)(2,1)}), bf16[8,1,2,256,128]{4,3,2,1,0:T(8,128)(2,1)}, u32[]{:S(2)}, u32[]{:S(2)}) %all-to-all-start) | async-done | bytes 1048608 | tf_op jit(solution)/shard_map/all_to_all | solution.py:172
  23.4 9.2 %lse.1 = (f32[8,256]{1,0:T(8,128)}, f32[8,256]{1,0:T(8,128)}) custom-call(s32[13]{0:T(128)} %concatenate.147.table, bf16[8,256,128]{2,1,0:T(8,128)(2,1)} %bitcast.65, bf16[8,256,128]{2,1,0:T(8,128)(2,1)} %collective-permute-done.refs_1_, bf16[8,2,256,128]{3,2,1,0:T(8,128)(2,1)} %bitcast.17.refs_2_.refs_8_), custom_call_target="tpu_custom_call" | custom-call | flops 1073741824 | bytes 1048576 | tf_op jit(solution)/shard_map/lse/pallas_call | solution.py:81
  32.6 0.0 collective-permute-done.2.refs_7_
  32.6 0.0 copy-start.4
  32.7 0.0 collective-permute-done.1.refs_3_
  32.7 0.6 copy-done.4
  33.2 26.2 %grads.1 = (bf16[8,8,64,128]{3,2,1,0:T(8,128)(2,1)}, bf16[8,2,64,128]{3,2,1,0:T(8,128)(2,1)}, bf16[8,2,64,128]{3,2,1,0:T(8,128)(2,1)}, bf16[8,2,64,128]{3,2,1,0:T(8,128)(2,1)}, bf16[8,2,64,128]{3,2,1,0:T(8,128)(2,1)}) custom-call(s32[13]{0:T(128)} %concatenate.147.table, bf16[8,256,128]{2,1,0:T(8,128)(2,1)} %bitcast.66, ...), custom_call_target="tpu_custom_call" | custom-call | flops 5368709120 | bytes 3145728 | tf_op jit(solution)/shard_map/grads/pallas_call | solution.py:155
  59.4 0.0 collective-permute-start.3
  59.4 1.2 %collective-permute-start.4 = (bf16[8,2,64,128]{3,2,1,0:T(8,128)(2,1)}, bf16[8,2,64,128]{3,2,1,0:T(8,128)(2,1)S(1)}, u32[]{:S(2)}, u32[]{:S(2)}) collective-permute-start(bf16[8,2,64,128]{3,2,1,0:T(8,128)(2,1)} %get-tuple-element.15), channel_id=1, source_target_pairs={{0,2},{1,3},{2,0},{3,1},{4,6},{5,7},{6,4},{7,5},{8,10},{9,11},{10,... | collective-permute-start | bytes 786440 | tf_op jit(solution)/shard_map/ppermute | solution.py:183
  60.6 2.3 %collective-permute-start.5 = (bf16[8,2,64,128]{3,2,1,0:T(8,128)(2,1)}, bf16[8,2,64,128]{3,2,1,0:T(8,128)(2,1)S(1)}, u32[]{:S(2)}, u32[]{:S(2)}) collective-permute-start(bf16[8,2,64,128]{3,2,1,0:T(8,128)(2,1)} %get-tuple-element.16), channel_id=1, source_target_pairs={{0,3},{1,2},{2,1},{3,0},{4,7},{5,6},{6,5},{7,4},{8,11},{9,10},{10,... | collective-permute-start | bytes 786440 | tf_op jit(solution)/shard_map/ppermute | solution.py:183
  62.9 0.0 copy-start.3
  62.9 5.5 %all-to-all-start.1 = ((bf16[8,8,64,128]{3,2,1,0:T(8,128)(2,1)}), bf16[8,8,64,128]{3,2,1,0:T(8,128)(2,1)S(1)}, u32[]{:S(2)}, u32[]{:S(2)}) async-start(bf16[8,8,64,128]{3,2,1,0:T(8,128)(2,1)} %get-tuple-element.12), calls=%async_computation.1 | async-start | bytes 2097152 | tf_op jit(solution)/shard_map/all_to_all | solution.py:172
  68.4 0.4 collective-permute-done.3
  68.8 5.1 %collective-permute-done.4 = bf16[8,2,64,128]{3,2,1,0:T(8,128)(2,1)S(1)} collective-permute-done((bf16[8,2,64,128]{3,2,1,0:T(8,128)(2,1)}, bf16[8,2,64,128]{3,2,1,0:T(8,128)(2,1)S(1)}, u32[]{:S(2)}, u32[]{:S(2)}) %collective-permute-start.4) | collective-permute-done | bytes 262176 | tf_op jit(solution)/shard_map/ppermute | solution.py:183
  73.9 0.0 collective-permute-done.5
  73.9 0.0 copy-done.3
  73.9 0.2 add_convert_fusion
  74.1 0.1 collective-permute-start.12
  74.2 1.2 %collective-permute-done.12 = bf16[1,2,64,128]{3,2,1,0:T(8,128)(2,1)S(1)} collective-permute-done((bf16[1,2,64,128]{3,2,1,0:T(8,128)(2,1)S(1)}, bf16[1,2,64,128]{3,2,1,0:T(8,128)(2,1)S(1)}, u32[]{:S(2)}, u32[]{:S(2)}) %collective-permute-start.12) | collective-permute-done | bytes 32800 | tf_op jit(solution)/shard_map/ppermute | solution.py:264
  75.4 3.9 %collective-permute-start.6 = (bf16[1,2,64,128]{3,2,1,0:T(8,128)(2,1)S(1)}, bf16[1,2,64,128]{3,2,1,0:T(8,128)(2,1)S(1)}, u32[]{:S(2)}, u32[]{:S(2)}) collective-permute-start(bf16[1,2,64,128]{3,2,1,0:T(8,128)(2,1)S(1)} %get-tuple-element.38), channel_id=1, source_target_pairs={{0,28},{4,24},{8,20},{12,16},{16,12},{20,8},{24,4},{28,0},{1,29},{... | collective-permute-start | bytes 98312 | tf_op jit(solution)/shard_map/ppermute | solution.py:264
  79.3 0.3 collective-permute-start.7
  79.6 0.4 collective-permute-start.8
  80.0 2.2 %collective-permute-start.9 = (bf16[1,2,64,128]{3,2,1,0:T(8,128)(2,1)S(1)}, bf16[1,2,64,128]{3,2,1,0:T(8,128)(2,1)S(1)}, u32[]{:S(2)}, u32[]{:S(2)}) collective-permute-start(bf16[1,2,64,128]{3,2,1,0:T(8,128)(2,1)S(1)} %get-tuple-element.39), channel_id=1, source_target_pairs={{0,16},{4,20},{8,24},{12,28},{16,0},{20,4},{24,8},{28,12},{1,17},{... | collective-permute-start | bytes 98312 | tf_op jit(solution)/shard_map/ppermute | solution.py:264
  82.1 1.2 %collective-permute-start.10 = (bf16[1,2,64,128]{3,2,1,0:T(8,128)(2,1)S(1)}, bf16[1,2,64,128]{3,2,1,0:T(8,128)(2,1)S(1)}, u32[]{:S(2)}, u32[]{:S(2)}) collective-permute-start(bf16[1,2,64,128]{3,2,1,0:T(8,128)(2,1)S(1)} %get-tuple-element.42), channel_id=1, source_target_pairs={{0,12},{4,8},{8,4},{12,0},{16,28},{20,24},{24,20},{28,16},{1,13},{... | collective-permute-start | bytes 98312 | tf_op jit(solution)/shard_map/ppermute | solution.py:264
  83.4 7.2 %collective-permute-done.6 = bf16[1,2,64,128]{3,2,1,0:T(8,128)(2,1)S(1)} collective-permute-done((bf16[1,2,64,128]{3,2,1,0:T(8,128)(2,1)S(1)}, bf16[1,2,64,128]{3,2,1,0:T(8,128)(2,1)S(1)}, u32[]{:S(2)}, u32[]{:S(2)}) %collective-permute-start.6) | collective-permute-done | bytes 32800 | tf_op jit(solution)/shard_map/ppermute | solution.py:264
  90.6 7.9 %collective-permute-start.11 = (bf16[1,2,64,128]{3,2,1,0:T(8,128)(2,1)S(1)}, bf16[1,2,64,128]{3,2,1,0:T(8,128)(2,1)S(1)}, u32[]{:S(2)}, u32[]{:S(2)}) collective-permute-start(bf16[1,2,64,128]{3,2,1,0:T(8,128)(2,1)S(1)} %get-tuple-element.41), channel_id=1, source_target_pairs={{0,8},{4,12},{8,0},{12,4},{16,24},{20,28},{24,16},{28,20},{1,9},{5... | collective-permute-start | bytes 98312 | tf_op jit(solution)/shard_map/ppermute | solution.py:264
  98.5 0.0 collective-permute-done.7
  98.5 0.8 collective-permute-done.8
  99.3 1.3 %collective-permute-done.9 = bf16[1,2,64,128]{3,2,1,0:T(8,128)(2,1)S(1)} collective-permute-done((bf16[1,2,64,128]{3,2,1,0:T(8,128)(2,1)S(1)}, bf16[1,2,64,128]{3,2,1,0:T(8,128)(2,1)S(1)}, u32[]{:S(2)}, u32[]{:S(2)}) %collective-permute-start.9) | collective-permute-done | bytes 32800 | tf_op jit(solution)/shard_map/ppermute | solution.py:264
  100.6 0.0 collective-permute-done.10
  100.6 0.7 collective-permute-done.11
  101.6 0.7 copy.57
  102.3 0.7 copy.58
  103.1 0.0 all-to-all-done.1
  103.1 1.6 %copy.54 = bf16[64,4,2,8,128]{4,3,2,1,0:T(8,128)(2,1)} copy(bf16[64,4,2,8,128]{4,0,3,1,2:T(8,128)(2,1)S(1)} %bitcast.61) | data formatting | bytes 2097152 | tf_op jit(solution)/shard_map/transpose | solution.py:253
  (15 shorter events, 0.3 us)
Async XLA Ops:
  3.2 5.3 %copy-start = (bf16[256,16,128]{2,1,0:T(8,128)(2,1)S(1)}, bf16[256,16,128]{2,1,0:T(8,128)(2,1)}, u32[]{:S(2)}) copy-start(bf16[256,16,128]{2,1,0:T(8,128)(2,1)} %param.10) | copy-start | bytes 3145732
  3.2 5.3 %copy-start.1 = (bf16[256,16,128]{2,1,0:T(8,128)(2,1)S(1)}, bf16[256,16,128]{2,1,0:T(8,128)(2,1)}, u32[]{:S(2)}) copy-start(bf16[256,16,128]{2,1,0:T(8,128)(2,1)} %param.6) | copy-start | bytes 3145732
  3.2 20.2 %all-to-all-start = ((bf16[8,1,2,256,128]{4,3,2,1,0:T(8,128)(2,1)}), bf16[8,1,2,256,128]{4,3,2,1,0:T(8,128)(2,1)}, u32[]{:S(2)}, u32[]{:S(2)}) async-start(bf16[8,1,2,256,128]{4,3,2,1,0:T(8,128)(2,1)} %bitcast.16), calls=%async_computation | async-start | bytes 2097152 | tf_op jit(solution)/shard_map/all_to_all | solution.py:172
  8.9 2.3 %copy-start.2 = (bf16[256,16,128]{2,1,0:T(8,128)(2,1)S(1)}, bf16[256,16,128]{2,1,0:T(8,128)(2,1)}, u32[]{:S(2)}) copy-start(bf16[256,16,128]{2,1,0:T(8,128)(2,1)} %param.9) | copy-start | bytes 3145732
  9.8 5.9 %collective-permute-start = (bf16[8,256,128]{2,1,0:T(8,128)(2,1)}, bf16[8,256,128]{2,1,0:T(8,128)(2,1)}, u32[]{:S(2)}, u32[]{:S(2)}) collective-permute-start(bf16[8,256,128]{2,1,0:T(8,128)(2,1)} %bitcast.58), channel_id=1, source_target_pairs={{0,4},{4,0},{1,5},{5,1},{2,6},{6,2},{3,7},{7,3},{8,12},{12,8},{9,1... | collective-permute-start | bytes 1572872 | tf_op jit(solution)/shard_map/ppermute | solution.py:223
  11.2 21.5 %collective-permute-start.1 = (bf16[8,256,128]{2,1,0:T(8,128)(2,1)}, bf16[8,256,128]{2,1,0:T(8,128)(2,1)}, u32[]{:S(2)}, u32[]{:S(2)}) collective-permute-start(bf16[8,256,128]{2,1,0:T(8,128)(2,1)} %bitcast.56), channel_id=1, source_target_pairs={{0,4},{4,0},{1,5},{5,1},{2,6},{6,2},{3,7},{7,3},{8,12},{12,8},{9,1... | collective-permute-start | bytes 1572872 | tf_op jit(solution)/shard_map/ppermute | solution.py:223
  12.5 20.1 %collective-permute-start.2 = (f32[8,256]{1,0:T(8,128)S(1)}, f32[8,256]{1,0:T(8,128)S(1)}, u32[]{:S(2)}, u32[]{:S(2)}) collective-permute-start(f32[8,256]{1,0:T(8,128)S(1)} %get-tuple-element.49), channel_id=1, source_target_pairs={{0,4},{4,0},{1,5},{5,1},{2,6},{6,2},{3,7},{7,3},{8,12},{12,8},{9,1... | collective-permute-start | bytes 24584 | tf_op jit(solution)/shard_map/ppermute | solution.py:223
  13.0 1.8 %copy-start.5 = (s32[1,8]{1,0:T(1,128)S(1)}, s32[1,8]{1,0:T(1,128)}, u32[]{:S(2)}) copy-start(s32[1,8]{1,0:T(1,128)} %param.11) | copy-start | bytes 100
  32.6 0.6 copy-start.4
  59.4 9.4 %collective-permute-start.3 = (bf16[8,2,64,128]{3,2,1,0:T(8,128)(2,1)}, bf16[8,2,64,128]{3,2,1,0:T(8,128)(2,1)S(1)}, u32[]{:S(2)}, u32[]{:S(2)}) collective-permute-start(bf16[8,2,64,128]{3,2,1,0:T(8,128)(2,1)} %get-tuple-element.14), channel_id=1, source_target_pairs={{0,1},{1,0},{2,3},{3,2},{4,5},{5,4},{6,7},{7,6},{8,9},{9,8},{10,11... | collective-permute-start | bytes 786440 | tf_op jit(solution)/shard_map/ppermute | solution.py:183
  59.4 14.5 %collective-permute-start.4 = (bf16[8,2,64,128]{3,2,1,0:T(8,128)(2,1)}, bf16[8,2,64,128]{3,2,1,0:T(8,128)(2,1)S(1)}, u32[]{:S(2)}, u32[]{:S(2)}) collective-permute-start(bf16[8,2,64,128]{3,2,1,0:T(8,128)(2,1)} %get-tuple-element.15), channel_id=1, source_target_pairs={{0,2},{1,3},{2,0},{3,1},{4,6},{5,7},{6,4},{7,5},{8,10},{9,11},{10,... | collective-permute-start | bytes 786440 | tf_op jit(solution)/shard_map/ppermute | solution.py:183
  60.6 13.3 %collective-permute-start.5 = (bf16[8,2,64,128]{3,2,1,0:T(8,128)(2,1)}, bf16[8,2,64,128]{3,2,1,0:T(8,128)(2,1)S(1)}, u32[]{:S(2)}, u32[]{:S(2)}) collective-permute-start(bf16[8,2,64,128]{3,2,1,0:T(8,128)(2,1)} %get-tuple-element.16), channel_id=1, source_target_pairs={{0,3},{1,2},{2,1},{3,0},{4,7},{5,6},{6,5},{7,4},{8,11},{9,10},{10,... | collective-permute-start | bytes 786440 | tf_op jit(solution)/shard_map/ppermute | solution.py:183
  62.9 11.0 %copy-start.3 = (bf16[8,2,64,128]{3,2,1,0:T(8,128)(2,1)S(1)}, bf16[8,2,64,128]{3,2,1,0:T(8,128)(2,1)}, u32[]{:S(2)}) copy-start(bf16[8,2,64,128]{3,2,1,0:T(8,128)(2,1)} %get-tuple-element.13) | copy-start | bytes 786436
  62.9 40.1 %all-to-all-start.1 = ((bf16[8,8,64,128]{3,2,1,0:T(8,128)(2,1)}), bf16[8,8,64,128]{3,2,1,0:T(8,128)(2,1)S(1)}, u32[]{:S(2)}, u32[]{:S(2)}) async-start(bf16[8,8,64,128]{3,2,1,0:T(8,128)(2,1)} %get-tuple-element.12), calls=%async_computation.1 | async-start | bytes 2097152 | tf_op jit(solution)/shard_map/all_to_all | solution.py:172
  74.1 1.3 %collective-permute-start.12 = (bf16[1,2,64,128]{3,2,1,0:T(8,128)(2,1)S(1)}, bf16[1,2,64,128]{3,2,1,0:T(8,128)(2,1)S(1)}, u32[]{:S(2)}, u32[]{:S(2)}) collective-permute-start(bf16[1,2,64,128]{3,2,1,0:T(8,128)(2,1)S(1)} %slice.56), channel_id=1, source_target_pairs={{0,4},{4,0},{8,12},{12,8},{16,20},{20,16},{24,28},{28,24},{1,5},{5... | collective-permute-start | bytes 98312 | tf_op jit(solution)/shard_map/ppermute | solution.py:264
  75.4 15.2 %collective-permute-start.6 = (bf16[1,2,64,128]{3,2,1,0:T(8,128)(2,1)S(1)}, bf16[1,2,64,128]{3,2,1,0:T(8,128)(2,1)S(1)}, u32[]{:S(2)}, u32[]{:S(2)}) collective-permute-start(bf16[1,2,64,128]{3,2,1,0:T(8,128)(2,1)S(1)} %get-tuple-element.38), channel_id=1, source_target_pairs={{0,28},{4,24},{8,20},{12,16},{16,12},{20,8},{24,4},{28,0},{1,29},{... | collective-permute-start | bytes 98312 | tf_op jit(solution)/shard_map/ppermute | solution.py:264
  79.3 19.2 %collective-permute-start.7 = (bf16[1,2,64,128]{3,2,1,0:T(8,128)(2,1)S(1)}, bf16[1,2,64,128]{3,2,1,0:T(8,128)(2,1)S(1)}, u32[]{:S(2)}, u32[]{:S(2)}) collective-permute-start(bf16[1,2,64,128]{3,2,1,0:T(8,128)(2,1)S(1)} %get-tuple-element.37), channel_id=1, source_target_pairs={{0,24},{4,28},{8,16},{12,20},{16,8},{20,12},{24,0},{28,4},{1,25},{... | collective-permute-start | bytes 98312 | tf_op jit(solution)/shard_map/ppermute | solution.py:264
  79.6 19.8 %collective-permute-start.8 = (bf16[1,2,64,128]{3,2,1,0:T(8,128)(2,1)S(1)}, bf16[1,2,64,128]{3,2,1,0:T(8,128)(2,1)S(1)}, u32[]{:S(2)}, u32[]{:S(2)}) collective-permute-start(bf16[1,2,64,128]{3,2,1,0:T(8,128)(2,1)S(1)} %get-tuple-element.40), channel_id=1, source_target_pairs={{0,20},{4,16},{8,28},{12,24},{16,4},{20,0},{24,12},{28,8},{1,21},{... | collective-permute-start | bytes 98312 | tf_op jit(solution)/shard_map/ppermute | solution.py:264
  80.0 20.7 %collective-permute-start.9 = (bf16[1,2,64,128]{3,2,1,0:T(8,128)(2,1)S(1)}, bf16[1,2,64,128]{3,2,1,0:T(8,128)(2,1)S(1)}, u32[]{:S(2)}, u32[]{:S(2)}) collective-permute-start(bf16[1,2,64,128]{3,2,1,0:T(8,128)(2,1)S(1)} %get-tuple-element.39), channel_id=1, source_target_pairs={{0,16},{4,20},{8,24},{12,28},{16,0},{20,4},{24,8},{28,12},{1,17},{... | collective-permute-start | bytes 98312 | tf_op jit(solution)/shard_map/ppermute | solution.py:264
  82.1 18.5 %collective-permute-start.10 = (bf16[1,2,64,128]{3,2,1,0:T(8,128)(2,1)S(1)}, bf16[1,2,64,128]{3,2,1,0:T(8,128)(2,1)S(1)}, u32[]{:S(2)}, u32[]{:S(2)}) collective-permute-start(bf16[1,2,64,128]{3,2,1,0:T(8,128)(2,1)S(1)} %get-tuple-element.42), channel_id=1, source_target_pairs={{0,12},{4,8},{8,4},{12,0},{16,28},{20,24},{24,20},{28,16},{1,13},{... | collective-permute-start | bytes 98312 | tf_op jit(solution)/shard_map/ppermute | solution.py:264
  90.6 10.8 %collective-permute-start.11 = (bf16[1,2,64,128]{3,2,1,0:T(8,128)(2,1)S(1)}, bf16[1,2,64,128]{3,2,1,0:T(8,128)(2,1)S(1)}, u32[]{:S(2)}, u32[]{:S(2)}) collective-permute-start(bf16[1,2,64,128]{3,2,1,0:T(8,128)(2,1)S(1)} %get-tuple-element.41), channel_id=1, source_target_pairs={{0,8},{4,12},{8,0},{12,4},{16,24},{20,28},{24,16},{28,20},{1,9},{5... | collective-permute-start | bytes 98312 | tf_op jit(solution)/shard_map/ppermute | solution.py:264
where the time goes:
time: 105 us
  Pallas kernels  35.4 us (34%)
  starting transfers between devices  31.3 us (30%)
  waiting for transfers between devices  24.3 us (23%)
  local copies, waits for them, and re-layouts  10.2 us (10%)
  other arithmetic  2.65 us (3%)
    pallas_call x1, Pallas kernels, grad_call(): pl.pallas_call(functools.partial(grad_kernel, group, scale, inner, slots)...  26.2 us
    ppermute x7, starting transfers between devices, body(): pieces[z][c] = lax.ppermute(pieces[z][c], ('head', 'outer'), pairs)  16 us
    ppermute x7, waiting for transfers between devices, body(): pieces[z][c] = lax.ppermute(pieces[z][c], ('head', 'outer'), pairs)  11.1 us
    all_to_all x2, starting transfers between devices, exchange(): return lax.all_to_all(x, axes, split_axis=0, concat_axis=0, tiled=True)  10.8 us
    pallas_call x1, Pallas kernels, lse_call(): pl.pallas_call(functools.partial(lse_kernel, group, scale, blocks), out_s...  9.24 us
    all_to_all x2, waiting for transfers between devices, exchange(): return lax.all_to_all(x, axes, split_axis=0, concat_axis=0, tiled=True)  7.64 us
    unnamed x18, local copies, waits for them, and re-layouts  5.61 us
    ppermute x3, waiting for transfers between devices, trade(): lax.ppermute(x, axis, [(d, partner(d, step, count)) for d in range(count)])  5.51 us
  transfers between devices with their start and end apart: 15, of which 8 were waited for; matrix products, arithmetic and copies ran while one was open for 8% of the time, Pallas kernels for 9%

commit v1 on v0

v1 whole, which is shorter than its diff:
```python
import functools
import math

import jax
import jax.numpy as jnp
from jax import lax
from jax.experimental import pallas as pl
from jax.experimental.pallas import tpu as pltpu
from jax.sharding import PartitionSpec as P


F32 = jnp.float32
BF16 = jnp.bfloat16
NT = (((1,), (1,)), ((), ()))
NN = (((1,), (0,)), ((), ()))
MASKED = -1e30
VMEM = pl.BlockSpec(memory_space=pltpu.VMEM)
SMEM = pl.BlockSpec(memory_space=pltpu.SMEM)


def dot(a, b, dims):
    return lax.dot_general(a, b, dims, preferred_element_type=F32)


def causal_tile(rows):
    shape = (rows, rows)
    return lax.broadcasted_iota(jnp.int32, shape, 0) <= lax.broadcasted_iota(jnp.int32, shape, 1)


def over_visible(place, tile):
    tile(place, True)

    def turn(k, _):
        tile(k, False)
        return 0

    lax.fori_loop(0, place, turn, 0)


def grad_kernel(group, chunk, scale, slots, inner, table, *refs):
    q_refs, do_refs, delta_refs = (refs[k * slots : (k + 1) * slots] for k in range(3))
    kv_ref, dq_ref = refs[3 * slots], refs[3 * slots + 1]
    out_refs = refs[3 * slots + 2 : -9]
    kt_ref, x_ref, m_ref, l_ref, dqt_ref, dka_ref, dva_ref, p_ref, ds_ref = refs[-9:]
    heads, rows, width = q_refs[0].shape
    blocks = kv_ref.shape[0]
    slice_rows = dq_ref.shape[2]
    zs = rows // slice_rows
    scale2 = scale * math.log2(math.e)
    causal = causal_tile(rows)
    core, place_in, z_in = (table[blocks + slots + k] for k in range(3))
    dka_ref[...] = jnp.zeros_like(dka_ref)
    dva_ref[...] = jnp.zeros_like(dva_ref)
    for b in range(blocks):
        kt_ref[b] = kv_ref[b, 0].T
    for s in range(slots):
        q_ref, do_ref, delta_ref = q_refs[s], do_refs[s], delta_refs[s]
        place = table[blocks + s]
        for g in range(0, heads, group):

            def totals(k, diag):
                keys = kv_ref[table[k], 0]
                for j in range(group):
                    x = dot(keys, q_ref[g + j], NT) * scale2
                    if diag:
                        x = jnp.where(causal, x, MASKED)
                    x_ref[k, j] = x
                    x = x.reshape(rows // 8, 8, rows)
                    m_new = jnp.max(x, axis=0)
                    if not diag:
                        m_old = m_ref[j]
                        m_new = jnp.maximum(m_old, m_new)
                    total = jnp.sum(jnp.exp2(x - m_new[None]), axis=0)
                    if not diag:
                        total = total + l_ref[j] * jnp.exp2(m_old - m_new)
                    m_ref[j] = m_new
                    l_ref[j] = total

            over_visible(place, totals)
            for j in range(group):
                m = m_ref[j]
                high = jnp.max(m, axis=0, keepdims=True)
                total = jnp.sum(l_ref[j] * jnp.exp2(m - high), axis=0, keepdims=True)
                m_ref[j] = jnp.broadcast_to(high + jnp.log2(total), (8, rows))

            def tile(k, diag):
                block = table[k]
                for j in range(group):
                    lse_row, delta_row = m_ref[j, 0:1], delta_ref[g + j : g + j + 1, :]
                    head = slice(j * rows, (j + 1) * rows)
                    for c in range(0, rows, chunk):
                        cut = slice(c, c + chunk)
                        dp = dot(kv_ref[block, 1, cut], do_ref[g + j], NT)
                        p = jnp.exp2(x_ref[k, j, cut] - lse_row)
                        p_ref[cut, head] = p.astype(BF16)
                        ds_ref[cut, head] = (p * (dp - delta_row)).astype(BF16)
                keys_t = kt_ref[block]
                for j in range(group):
                    part = dot(keys_t, ds_ref[:, j * rows : (j + 1) * rows], NN)
                    if diag:
                        dqt_ref[j] = part
                    else:
                        dqt_ref[j] += part
                wide = slice(g, g + group)
                dva_ref[block] += dot(p_ref[...], do_ref[wide].reshape(group * rows, width), NN)
                dka_ref[block] += dot(ds_ref[...], q_ref[wide].reshape(group * rows, width), NN)

            over_visible(place, tile)
            to_core = lax.rem(core + s, slots)
            for j in range(group):
                dq = (dqt_ref[j] * scale).T.astype(BF16)
                for z in range(zs):
                    dq_ref[to_core * zs + z, g + j] = dq[z * slice_rows : (z + 1) * slice_rows]
    for step, out_ref in enumerate(out_refs):
        block = partner(core, step // inner, slots) * inner + partner(place_in, step % inner, inner)
        for z in range(zs):
            start = pl.multiple_of(partner(z_in, z, zs) * slice_rows, slice_rows)
            cut = pl.ds(start, slice_rows)
            out_ref[z, 0] = (dka_ref[block, cut] * scale).astype(BF16)
            out_ref[z, 1] = dva_ref[block, cut].astype(BF16)


def grad_call(table, q, do, delta, kv, group, scale, inner, zs):
    heads, rows, width = q[0].shape
    slots, blocks = len(q), kv.shape[0]
    slice_rows = rows // zs
    chunk = rows // 2
    flops = 5 * slots * heads * rows * rows * blocks * width
    outs = [(slots * zs, heads, slice_rows, width)] + [(zs, 2, slice_rows, width)] * blocks
    return pl.pallas_call(
        functools.partial(grad_kernel, group, chunk, scale, slots, inner),
        out_shape=[jax.ShapeDtypeStruct(shape, BF16) for shape in outs],
        in_specs=[SMEM] + [VMEM] * (3 * slots + 1),
        out_specs=[VMEM] * len(outs),
        scratch_shapes=[
            pltpu.VMEM((blocks, width, rows), BF16),
            pltpu.VMEM((blocks, group, rows, rows), F32),
            pltpu.VMEM((group, 8, rows), F32),
            pltpu.VMEM((group, 8, rows), F32),
            pltpu.VMEM((group, width, rows), F32),
            pltpu.VMEM((blocks, rows, width), F32),
            pltpu.VMEM((blocks, rows, width), F32),
            pltpu.VMEM((rows, group * rows), BF16),
            pltpu.VMEM((rows, group * rows), BF16),
        ],
        cost_estimate=pl.CostEstimate(flops=flops, bytes_accessed=q[0].size * 12, transcendentals=0),
        name="grads",
    )(table, *q, *do, *delta, kv)


def exchange(x, axes):
    return lax.all_to_all(x, axes, split_axis=0, concat_axis=0, tiled=True)


def partner(index, step, count):
    if count & (count - 1) == 0:
        return index ^ step
    return (step - index) % count


def trade(x, axes, steps):
    counts = [lax.axis_size(axis) for axis in axes]
    pairs = []
    for device in range(math.prod(counts)):
        target, rest = 0, device
        places = []
        for count in reversed(counts):
            places.insert(0, rest % count)
            rest //= count
        for spot, step, count in zip(places, steps, counts):
            target = target * count + partner(spot, step, count)
        pairs.append((device, target))
    return lax.ppermute(x, axes, pairs)


def natural(pieces, index):
    count = len(pieces)

    def pick(place):
        kept = pieces[0]
        for step in range(1, count):
            kept = jnp.where(partner(index, step, count) == place, pieces[step], kept)
        return kept

    return [pick(place) for place in range(count)]


def body(query, keys, values, forward_output, d_out, span_order):
    rows, heads, width = query.shape
    kv_count = keys.shape[1]
    scale = width ** (-0.5)
    cores, inner, zs = lax.axis_size("outer"), lax.axis_size("inner"), lax.axis_size("head")
    core, place, z_in = (lax.axis_index(axis) for axis in ("outer", "inner", "head"))
    blocks = cores * inner
    own_heads = heads // cores
    shared = kv_count % cores != 0
    own_kv = 1 if shared else kv_count // cores
    group_heads = own_heads // own_kv
    slice_rows = rows // zs
    group = max(1, min(8, group_heads, 64 // blocks))

    kv = jnp.stack([jnp.moveaxis(keys, 1, 0), jnp.moveaxis(values, 1, 0)], axis=1)
    kv = jnp.broadcast_to(kv, (cores,) + kv.shape) if shared else kv.reshape((cores, own_kv) + kv.shape[1:])
    kv = jnp.broadcast_to(kv[:, None], (cores, inner) + kv.shape[1:])
    kv = exchange(kv.reshape((blocks,) + kv.shape[2:]), ("outer", "inner"))

    def share(x):
        x = jnp.moveaxis(x, 1, 0)
        x = x.reshape((cores, own_heads) + x.shape[1:])
        got = [lax.dynamic_index_in_dim(x, core, 0, keepdims=False)]
        for step in range(1, cores):
            out = lax.dynamic_index_in_dim(x, (core + step) % cores, 0, keepdims=False)
            got.append(lax.ppermute(out, "outer", [(d, (d + step) % cores) for d in range(cores)]))
        return [got[0]] + got[:0:-1]

    delta = jnp.sum(d_out.astype(F32) * forward_output.astype(F32), axis=-1)
    q_all, do_all, delta_all = share(query), share(d_out), share(delta)

    order = span_order[0]
    ids = jnp.arange(blocks, dtype=jnp.int32)
    by_place = jnp.sum(jnp.where(order[None, :] == ids[:, None], ids[None, :], 0), axis=1)
    own_blocks = (core + jnp.arange(cores, dtype=jnp.int32)) % cores * inner + place
    places = jnp.sum(jnp.where(own_blocks[:, None] == ids[None, :], order[None, :], 0), axis=1)
    table = jnp.concatenate([by_place, places, jnp.stack([core, place, z_in]).astype(jnp.int32)])

    dq, pieces = [], []
    for g in range(own_kv):
        mine = slice(g * group_heads, (g + 1) * group_heads)
        q, do, delta_g = ([part[mine] for part in x] for x in (q_all, do_all, delta_all))
        dq_g, *pieces_g = grad_call(table, q, do, delta_g, kv[:, g], group, scale, inner, zs)
        dq.append(dq_g)
        pieces.append(pieces_g)
    pieces = [jnp.stack(part, axis=1) for part in zip(*pieces)]

    sums = [None] * cores
    for step, part in enumerate(pieces):
        c, i = divmod(step, inner)
        if step:
            part = trade(part, ("outer", "inner"), (c, i))
        part = part.astype(F32)
        sums[c] = part if sums[c] is None else sums[c] + part
    if shared:
        sums = [sum(sums)]
    else:
        sums = natural(sums, core)
    sums = jnp.concatenate(sums, axis=1).astype(BF16)

    dq = exchange(jnp.concatenate(dq, axis=1), ("outer", "head"))
    dq = dq.reshape(cores, zs, own_heads, slice_rows, width)
    dq = jnp.transpose(dq, (3, 1, 0, 2, 4)).reshape(1, slice_rows, zs * heads, width)
    got = [sums[0]]
    for z in range(1, zs):
        got.append(trade(sums[z], ("head",), (z,)))
    sums = jnp.stack(natural(got, z_in))
    sums = jnp.transpose(sums, (2, 3, 0, 1, 4)).reshape(2, 1, slice_rows, zs * kv_count, width)
    return dq, sums[0], sums[1]


def solution(mesh):
    rows_spec = P(("outer", "inner"), "head", None)
    out_spec = P(("outer", "inner"), "head", None, None)
    return jax.shard_map(
        body,
        mesh=mesh,
        in_specs=(rows_spec,) * 5 + (P(),),
        out_specs=(out_spec,) * 3,
        check_vma=False,
    )
```

time: 105 us -> 90.4 us (0.86)
  Pallas kernels: 35.4 us -> 25.6 us
  starting transfers between devices: 31.3 us -> 22 us
  waiting for transfers between devices: 24.3 us -> 29.4 us
    pallas_call x2 -> x1, Pallas kernels: 35.4 us -> 25.6 us  [grad_call(): pl.pallas_call(functools.partial(grad_kernel, group, chunk, scale, slots,...]
    ppermute x10, starting transfers between devices: 19.5 us -> 10.2 us  [trade(): return lax.ppermute(x, axes, pairs)]
    ppermute x10, waiting for transfers between devices: 16.7 us -> 21.8 us  [trade(): return lax.ppermute(x, axes, pairs)]
    unnamed x18 -> x32, local copies, waits for them, and re-layouts: 5.61 us -> 5.09 us
  transfers between devices with their start and end apart: 15 -> 15, of which waited for: 8 -> 7; matrix products, arithmetic and copies ran while one was open for 8% -> 9% of each run, Pallas kernels for 9% -> 0%
where the time goes in v1:
time: 90.4 us; the launch traced here: 90.1 us
  waiting for transfers between devices  29.4 us (33%)
  Pallas kernels  25.6 us (28%)
  starting transfers between devices  22 us (24%)
  local copies, waits for them, and re-layouts  9.68 us (11%)
  other arithmetic  2.58 us (3%)
    pallas_call x1, Pallas kernels, grad_call(): pl.pallas_call(functools.partial(grad_kernel, group, chunk, scale, slots,...  25.6 us
    ppermute x10, waiting for transfers between devices, trade(): return lax.ppermute(x, axes, pairs)  21.8 us
    all_to_all x2, starting transfers between devices, exchange(): return lax.all_to_all(x, axes, split_axis=0, concat_axis=0, tiled=True)  10.8 us
    ppermute x10, starting transfers between devices, trade(): return lax.ppermute(x, axes, pairs)  10.2 us
    all_to_all x2, waiting for transfers between devices, exchange(): return lax.all_to_all(x, axes, split_axis=0, concat_axis=0, tiled=True)  7.59 us
    unnamed x32, local copies, waits for them, and re-layouts  5.09 us
  transfers between devices with their start and end apart: 15, of which 7 were waited for; matrix products, arithmetic and copies ran while one was open for 9% of the time, Pallas kernels for 0%

profile of v1, /device:TPU:0, one launch (start us, length us, event | category | flops | bytes accessed | tf_op | source)
XLA Modules:
  0.0 90.1 jit_solution(13625941889568766781)
XLA Ops:
  0.6 1.4 %pad_maximum_fusion = bf16[2,2,256,128]{3,0,2,1:T(2,128)(2,1)S(1)} fusion(bf16[2,1,256,128]{3,0,2,1:T(2,128)(2,1)} %bitcast.90, bf16[2,1,256,128]{3,0,2,1:T(2,128)(2,1)} %bitcast.91), kind=kLoop, calls=%fused_computation.11 | loop fusion | flops 131072 | bytes 524288 | tf_op jit(solution)/shard_map/stack | solution.py:202
  2.0 1.2 %broadcast_in_dim.39 = bf16[2,4,2,256,128]{4,3,2,1,0:T(8,128)(2,1)} broadcast(bf16[2,2,256,128]{3,2,1,0:T(8,128)(2,1)S(1)} %copy.50), dimensions={0,2,3,4} | broadcast | bytes 1310720 | tf_op jit(solution)/shard_map/broadcast_in_dim | solution.py:204
  3.2 5.3 %all-to-all-start = ((bf16[8,1,2,256,128]{4,3,2,1,0:T(8,128)(2,1)}), bf16[8,1,2,256,128]{4,3,2,1,0:T(8,128)(2,1)}, u32[]{:S(2)}, u32[]{:S(2)}) async-start(bf16[8,1,2,256,128]{4,3,2,1,0:T(8,128)(2,1)} %bitcast.20), calls=%async_computation | async-start | bytes 2097152 | tf_op jit(solution)/shard_map/all_to_all | solution.py:152
  8.5 0.0 copy-done
  8.6 0.0 copy-done.1
  8.6 0.4 constant_dynamic-slice_fusion
  8.9 0.0 copy-start.2
  9.0 0.9 copy.70
  9.8 0.5 collective-permute-start
  10.3 0.9 copy.68
  11.2 0.0 collective-permute-start.1
  11.2 0.0 copy-done.2
  11.2 0.6 multiply_reduce_fusion
  11.9 0.1 copy.49
  11.9 0.6 dynamic-slice_bitcast_fusion
  12.5 0.5 collective-permute-start.2
  13.0 0.0 copy-done.12
  13.1 0.2 fusion.9
  13.2 0.1 select_reduce_fusion
  13.4 0.9 copy.69
  14.3 0.9 copy.71
  15.1 0.7 concatenate.7.table
  15.8 0.0 collective-permute-done.2.refs_5_
  15.8 0.0 collective-permute-done.refs_1_
  15.8 0.0 collective-permute-done.1.refs_3_
  15.8 7.6 %all-to-all-done = bf16[8,1,2,256,128]{4,3,2,1,0:T(8,128)(2,1)} async-done(((bf16[8,1,2,256,128]{4,3,2,1,0:T(8,128)(2,1)}), bf16[8,1,2,256,128]{4,3,2,1,0:T(8,128)(2,1)}, u32[]{:S(2)}, u32[]{:S(2)}) %all-to-all-start) | async-done | bytes 1048608 | tf_op jit(solution)/shard_map/all_to_all | solution.py:152
  23.4 0.0 copy-done.11
  23.4 25.6 %grads.1 = (bf16[8,8,64,128]{3,2,1,0:T(8,128)(2,1)}, bf16[4,2,64,128]{3,2,1,0:T(8,128)(2,1)}, bf16[4,2,64,128]{3,2,1,0:T(8,128)(2,1)}, bf16[4,2,64,128]{3,2,1,0:...) custom-call(s32[13]{0:T(128)} %concatenate.7.table, ...), custom_call_target="tpu_custom_call" | custom-call | flops 5368709120 | bytes 3145728 | tf_op jit(solution)/shard_map/grads/pallas_call | solution.py:130
  49.1 0.0 copy-start.8
  49.1 0.0 copy-start.7
  49.1 0.0 copy-start.6
  49.1 0.0 copy-start.5
  49.1 0.0 copy-start.4
  49.1 0.0 copy-start.3
  49.1 5.5 %all-to-all-start.1 = ((bf16[8,8,64,128]{3,2,1,0:T(8,128)(2,1)}), bf16[8,8,64,128]{3,2,1,0:T(8,128)(2,1)S(1)}, u32[]{:S(2)}, u32[]{:S(2)}) async-start(bf16[8,8,64,128]{3,2,1,0:T(8,128)(2,1)} %get-tuple-element.12), calls=%async_computation.1 | async-start | bytes 2097152 | tf_op jit(solution)/shard_map/all_to_all | solution.py:152
  54.6 0.0 copy-done.10
  54.6 0.5 collective-permute-start.3
  55.1 0.0 copy-done.9
  55.1 0.0 collective-permute-start.4
  55.1 0.0 copy-done.8
  55.1 0.9 collective-permute-start.5
  56.0 2.0 %collective-permute-start.6 = (bf16[4,1,2,64,128]{4,3,2,0,1:T(8,128)(2,1)S(1)}, bf16[4,1,2,64,128]{4,3,2,0,1:T(8,128)(2,1)S(1)}, u32[]{:S(2)}, u32[]{:S(2)}) collective-permute-start(bf16[4,1,2,64,128]{4,3,2,0,1:T(8,128)(2,1)S(1)} %bitcast.96), channel_id=1, source_target_pairs={{0,7},{1,6},{2,5},{3,4},{4,3},{5,2},{6,1},{7,0},{8,15},{9,14},{10,... | collective-permute-start | bytes 393224 | tf_op jit(solution)/shard_map/ppermute | solution.py:173
  58.0 0.4 collective-permute-start.7
  58.4 0.0 collective-permute-done.3
  58.4 0.0 copy-done.5
  58.4 1.1 %collective-permute-start.8 = (bf16[4,1,2,64,128]{4,3,2,0,1:T(8,128)(2,1)S(1)}, bf16[4,1,2,64,128]{4,3,2,0,1:T(8,128)(2,1)S(1)}, u32[]{:S(2)}, u32[]{:S(2)}) collective-permute-start(bf16[4,1,2,64,128]{4,3,2,0,1:T(8,128)(2,1)S(1)} %bitcast.94), channel_id=1, source_target_pairs={{0,2},{1,3},{2,0},{3,1},{4,6},{5,7},{6,4},{7,5},{8,10},{9,11},{10,... | collective-permute-start | bytes 393224 | tf_op jit(solution)/shard_map/ppermute | solution.py:173
  59.5 1.1 %collective-permute-done.4 = bf16[4,1,2,64,128]{4,3,2,0,1:T(8,128)(2,1)S(1)} collective-permute-done((bf16[4,1,2,64,128]{4,3,2,0,1:T(8,128)(2,1)S(1)}, bf16[4,1,2,64,128]{4,3,2,0,1:T(8,128)(2,1)S(1)}, u32[]{:S(2)}, u32[]{:S(2)}) %collective-permute-start.4) | collective-permute-done | bytes 131104 | tf_op jit(solution)/shard_map/ppermute | solution.py:173
  60.7 0.9 collective-permute-start.9
  61.5 0.0 collective-permute-done.5
  61.5 2.6 %collective-permute-done.6 = bf16[4,1,2,64,128]{4,3,2,0,1:T(8,128)(2,1)S(1)} collective-permute-done((bf16[4,1,2,64,128]{4,3,2,0,1:T(8,128)(2,1)S(1)}, bf16[4,1,2,64,128]{4,3,2,0,1:T(8,128)(2,1)S(1)}, u32[]{:S(2)}, u32[]{:S(2)}) %collective-permute-start.6) | collective-permute-done | bytes 131104 | tf_op jit(solution)/shard_map/ppermute | solution.py:173
  64.1 2.7 %collective-permute-done.7 = bf16[4,1,2,64,128]{4,3,2,0,1:T(8,128)(2,1)S(1)} collective-permute-done((bf16[4,1,2,64,128]{4,3,2,0,1:T(8,128)(2,1)S(1)}, bf16[4,1,2,64,128]{4,3,2,0,1:T(8,128)(2,1)S(1)}, u32[]{:S(2)}, u32[]{:S(2)}) %collective-permute-start.7) | collective-permute-done | bytes 131104 | tf_op jit(solution)/shard_map/ppermute | solution.py:173
  66.8 0.0 collective-permute-done.8
  66.8 3.1 %collective-permute-done.9 = bf16[4,1,2,64,128]{4,3,2,0,1:T(8,128)(2,1)S(1)} collective-permute-done((bf16[4,1,2,64,128]{4,3,2,0,1:T(8,128)(2,1)S(1)}, bf16[4,1,2,64,128]{4,3,2,0,1:T(8,128)(2,1)S(1)}, u32[]{:S(2)}, u32[]{:S(2)}) %collective-permute-start.9) | collective-permute-done | bytes 131104 | tf_op jit(solution)/shard_map/ppermute | solution.py:173
  69.9 0.2 select_convert_fusion
  70.1 3.5 %collective-permute-start.10 = (bf16[2,2,64,128]{3,2,1,0:T(8,128)(2,1)S(1)}, bf16[2,2,64,128]{3,2,1,0:T(8,128)(2,1)S(1)}, u32[]{:S(2)}, u32[]{:S(2)}) collective-permute-start(bf16[2,2,64,128]{3,2,1,0:T(8,128)(2,1)S(1)} %get-tuple-element.47), channel_id=1, source_target_pairs={{0,24},{8,16},{16,8},{24,0},{1,25},{9,17},{17,9},{25,1},{2,26},{10... | collective-permute-start | bytes 196616 | tf_op jit(solution)/shard_map/ppermute | solution.py:173
  73.6 0.0 collective-permute-start.11
  73.6 1.0 %collective-permute-start.12 = (bf16[2,2,64,128]{3,2,1,0:T(8,128)(2,1)S(1)}, bf16[2,2,64,128]{3,2,1,0:T(8,128)(2,1)S(1)}, u32[]{:S(2)}, u32[]{:S(2)}) collective-permute-start(bf16[2,2,64,128]{3,2,1,0:T(8,128)(2,1)S(1)} %get-tuple-element.46), channel_id=1, source_target_pairs={{0,8},{8,0},{16,24},{24,16},{1,9},{9,1},{17,25},{25,17},{2,10},{10... | collective-permute-start | bytes 196616 | tf_op jit(solution)/shard_map/ppermute | solution.py:173
  74.6 4.0 %collective-permute-done.10 = bf16[2,2,64,128]{3,2,1,0:T(8,128)(2,1)S(1)} collective-permute-done((bf16[2,2,64,128]{3,2,1,0:T(8,128)(2,1)S(1)}, bf16[2,2,64,128]{3,2,1,0:T(8,128)(2,1)S(1)}, u32[]{:S(2)}, u32[]{:S(2)}) %collective-permute-start.10) | collective-permute-done | bytes 65568 | tf_op jit(solution)/shard_map/ppermute | solution.py:173
  78.6 8.3 %collective-permute-done.11 = bf16[2,2,64,128]{3,2,1,0:T(8,128)(2,1)S(1)} collective-permute-done((bf16[2,2,64,128]{3,2,1,0:T(8,128)(2,1)S(1)}, bf16[2,2,64,128]{3,2,1,0:T(8,128)(2,1)S(1)}, u32[]{:S(2)}, u32[]{:S(2)}) %collective-permute-start.11) | collective-permute-done | bytes 65568 | tf_op jit(solution)/shard_map/ppermute | solution.py:173
  86.8 0.0 collective-permute-done.12
  87.0 0.7 copy.55
  87.7 0.7 copy.56
  88.5 0.0 all-to-all-done.1
  88.5 1.6 %copy.51 = bf16[64,4,2,8,128]{4,3,2,1,0:T(8,128)(2,1)} copy(bf16[64,4,2,8,128]{4,0,3,1,2:T(8,128)(2,1)S(1)} %bitcast.82) | data formatting | bytes 2097152 | tf_op jit(solution)/shard_map/transpose | solution.py:250
  (17 shorter events, 0.2 us)
Async XLA Ops:
  3.2 5.3 %copy-start = (bf16[256,16,128]{2,1,0:T(8,128)(2,1)S(1)}, bf16[256,16,128]{2,1,0:T(8,128)(2,1)}, u32[]{:S(2)}) copy-start(bf16[256,16,128]{2,1,0:T(8,128)(2,1)} %param.10) | copy-start | bytes 3145732
  3.2 5.3 %copy-start.1 = (bf16[256,16,128]{2,1,0:T(8,128)(2,1)S(1)}, bf16[256,16,128]{2,1,0:T(8,128)(2,1)}, u32[]{:S(2)}) copy-start(bf16[256,16,128]{2,1,0:T(8,128)(2,1)} %param.6) | copy-start | bytes 3145732
  3.2 20.2 %all-to-all-start = ((bf16[8,1,2,256,128]{4,3,2,1,0:T(8,128)(2,1)}), bf16[8,1,2,256,128]{4,3,2,1,0:T(8,128)(2,1)}, u32[]{:S(2)}, u32[]{:S(2)}) async-start(bf16[8,1,2,256,128]{4,3,2,1,0:T(8,128)(2,1)} %bitcast.20), calls=%async_computation | async-start | bytes 2097152 | tf_op jit(solution)/shard_map/all_to_all | solution.py:152
  8.9 2.3 %copy-start.2 = (bf16[256,16,128]{2,1,0:T(8,128)(2,1)S(1)}, bf16[256,16,128]{2,1,0:T(8,128)(2,1)}, u32[]{:S(2)}) copy-start(bf16[256,16,128]{2,1,0:T(8,128)(2,1)} %param.9) | copy-start | bytes 3145732
  9.8 6.0 %collective-permute-start = (bf16[8,256,128]{2,1,0:T(8,128)(2,1)}, bf16[8,256,128]{2,1,0:T(8,128)(2,1)}, u32[]{:S(2)}, u32[]{:S(2)}) collective-permute-start(bf16[8,256,128]{2,1,0:T(8,128)(2,1)} %bitcast.79), channel_id=1, source_target_pairs={{0,4},{4,0},{1,5},{5,1},{2,6},{6,2},{3,7},{7,3},{8,12},{12,8},{9,1... | collective-permute-start | bytes 1572872 | tf_op jit(solution)/shard_map/ppermute | solution.py:213
  11.2 1.8 %copy-start.12 = (s32[1,8]{1,0:T(1,128)S(1)}, s32[1,8]{1,0:T(1,128)}, u32[]{:S(2)}) copy-start(s32[1,8]{1,0:T(1,128)} %param.11) | copy-start | bytes 100
  11.2 4.6 %collective-permute-start.1 = (bf16[8,256,128]{2,1,0:T(8,128)(2,1)}, bf16[8,256,128]{2,1,0:T(8,128)(2,1)}, u32[]{:S(2)}, u32[]{:S(2)}) collective-permute-start(bf16[8,256,128]{2,1,0:T(8,128)(2,1)} %bitcast.77), channel_id=1, source_target_pairs={{0,4},{4,0},{1,5},{5,1},{2,6},{6,2},{3,7},{7,3},{8,12},{12,8},{9,1... | collective-permute-start | bytes 1572872 | tf_op jit(solution)/shard_map/ppermute | solution.py:213
  12.5 3.3 %collective-permute-start.2 = (f32[8,256]{1,0:T(8,128)S(1)}, f32[8,256]{1,0:T(8,128)S(1)}, u32[]{:S(2)}, u32[]{:S(2)}) collective-permute-start(f32[8,256]{1,0:T(8,128)S(1)} %get-tuple-element.49), channel_id=1, source_target_pairs={{0,4},{4,0},{1,5},{5,1},{2,6},{6,2},{3,7},{7,3},{8,12},{12,8},{9,1... | collective-permute-start | bytes 24584 | tf_op jit(solution)/shard_map/ppermute | solution.py:213
  15.8 7.6 %copy-start.11 = (f32[8,256]{1,0:T(8,128)}, f32[8,256]{1,0:T(8,128)S(1)}, u32[]{:S(2)}) copy-start(f32[8,256]{1,0:T(8,128)S(1)} %collective-permute-done.2.refs_5_) | copy-start | bytes 24580
  49.0 5.6 %copy-start.10 = (bf16[4,2,64,128]{3,2,1,0:T(8,128)(2,1)S(1)}, bf16[4,2,64,128]{3,2,1,0:T(8,128)(2,1)}, u32[]{:S(2)}) copy-start(bf16[4,2,64,128]{3,2,1,0:T(8,128)(2,1)} %get-tuple-element.13) | copy-start | bytes 393220
  49.1 6.1 %copy-start.9 = (bf16[4,2,64,128]{3,2,1,0:T(8,128)(2,1)S(1)}, bf16[4,2,64,128]{3,2,1,0:T(8,128)(2,1)}, u32[]{:S(2)}) copy-start(bf16[4,2,64,128]{3,2,1,0:T(8,128)(2,1)} %get-tuple-element.14) | copy-start | bytes 393220
  49.1 6.1 %copy-start.8 = (bf16[4,2,64,128]{3,2,1,0:T(8,128)(2,1)S(1)}, bf16[4,2,64,128]{3,2,1,0:T(8,128)(2,1)}, u32[]{:S(2)}) copy-start(bf16[4,2,64,128]{3,2,1,0:T(8,128)(2,1)} %get-tuple-element.15) | copy-start | bytes 393220
  49.1 6.9 %copy-start.7 = (bf16[4,2,64,128]{3,2,1,0:T(8,128)(2,1)S(1)}, bf16[4,2,64,128]{3,2,1,0:T(8,128)(2,1)}, u32[]{:S(2)}) copy-start(bf16[4,2,64,128]{3,2,1,0:T(8,128)(2,1)} %get-tuple-element.16) | copy-start | bytes 393220
  49.1 8.9 %copy-start.6 = (bf16[4,2,64,128]{3,2,1,0:T(8,128)(2,1)S(1)}, bf16[4,2,64,128]{3,2,1,0:T(8,128)(2,1)}, u32[]{:S(2)}) copy-start(bf16[4,2,64,128]{3,2,1,0:T(8,128)(2,1)} %get-tuple-element.18) | copy-start | bytes 393220
  49.1 9.3 %copy-start.5 = (bf16[4,2,64,128]{3,2,1,0:T(8,128)(2,1)S(1)}, bf16[4,2,64,128]{3,2,1,0:T(8,128)(2,1)}, u32[]{:S(2)}) copy-start(bf16[4,2,64,128]{3,2,1,0:T(8,128)(2,1)} %get-tuple-element.19) | copy-start | bytes 393220
  49.1 11.6 %copy-start.4 = (bf16[4,2,64,128]{3,2,1,0:T(8,128)(2,1)S(1)}, bf16[4,2,64,128]{3,2,1,0:T(8,128)(2,1)}, u32[]{:S(2)}) copy-start(bf16[4,2,64,128]{3,2,1,0:T(8,128)(2,1)} %get-tuple-element.20) | copy-start | bytes 393220
  49.1 20.8 %copy-start.3 = (bf16[4,2,64,128]{3,2,1,0:T(8,128)(2,1)S(1)}, bf16[4,2,64,128]{3,2,1,0:T(8,128)(2,1)}, u32[]{:S(2)}) copy-start(bf16[4,2,64,128]{3,2,1,0:T(8,128)(2,1)} %get-tuple-element.17) | copy-start | bytes 393220
  49.1 39.3 %all-to-all-start.1 = ((bf16[8,8,64,128]{3,2,1,0:T(8,128)(2,1)}), bf16[8,8,64,128]{3,2,1,0:T(8,128)(2,1)S(1)}, u32[]{:S(2)}, u32[]{:S(2)}) async-start(bf16[8,8,64,128]{3,2,1,0:T(8,128)(2,1)} %get-tuple-element.12), calls=%async_computation.1 | async-start | bytes 2097152 | tf_op jit(solution)/shard_map/all_to_all | solution.py:152
  54.6 3.8 %collective-permute-start.3 = (bf16[4,1,2,64,128]{4,3,2,0,1:T(8,128)(2,1)S(1)}, bf16[4,1,2,64,128]{4,3,2,0,1:T(8,128)(2,1)S(1)}, u32[]{:S(2)}, u32[]{:S(2)}) collective-permute-start(bf16[4,1,2,64,128]{4,3,2,0,1:T(8,128)(2,1)S(1)} %bitcast.99), channel_id=1, source_target_pairs={{0,4},{1,5},{2,6},{3,7},{4,0},{5,1},{6,2},{7,3},{8,12},{9,13},{10,... | collective-permute-start | bytes 393224 | tf_op jit(solution)/shard_map/ppermute | solution.py:173
  55.1 5.5 %collective-permute-start.4 = (bf16[4,1,2,64,128]{4,3,2,0,1:T(8,128)(2,1)S(1)}, bf16[4,1,2,64,128]{4,3,2,0,1:T(8,128)(2,1)S(1)}, u32[]{:S(2)}, u32[]{:S(2)}) collective-permute-start(bf16[4,1,2,64,128]{4,3,2,0,1:T(8,128)(2,1)S(1)} %bitcast.98), channel_id=1, source_target_pairs={{0,5},{1,4},{2,7},{3,6},{4,1},{5,0},{6,3},{7,2},{8,13},{9,12},{10,... | collective-permute-start | bytes 393224 | tf_op jit(solution)/shard_map/ppermute | solution.py:173
  55.1 6.4 %collective-permute-start.5 = (bf16[4,1,2,64,128]{4,3,2,0,1:T(8,128)(2,1)S(1)}, bf16[4,1,2,64,128]{4,3,2,0,1:T(8,128)(2,1)S(1)}, u32[]{:S(2)}, u32[]{:S(2)}) collective-permute-start(bf16[4,1,2,64,128]{4,3,2,0,1:T(8,128)(2,1)S(1)} %bitcast.97), channel_id=1, source_target_pairs={{0,6},{1,7},{2,4},{3,5},{4,2},{5,3},{6,0},{7,1},{8,14},{9,15},{10,... | collective-permute-start | bytes 393224 | tf_op jit(solution)/shard_map/ppermute | solution.py:173
  56.0 8.1 %collective-permute-start.6 = (bf16[4,1,2,64,128]{4,3,2,0,1:T(8,128)(2,1)S(1)}, bf16[4,1,2,64,128]{4,3,2,0,1:T(8,128)(2,1)S(1)}, u32[]{:S(2)}, u32[]{:S(2)}) collective-permute-start(bf16[4,1,2,64,128]{4,3,2,0,1:T(8,128)(2,1)S(1)} %bitcast.96), channel_id=1, source_target_pairs={{0,7},{1,6},{2,5},{3,4},{4,3},{5,2},{6,1},{7,0},{8,15},{9,14},{10,... | collective-permute-start | bytes 393224 | tf_op jit(solution)/shard_map/ppermute | solution.py:173
  58.0 8.8 %collective-permute-start.7 = (bf16[4,1,2,64,128]{4,3,2,0,1:T(8,128)(2,1)S(1)}, bf16[4,1,2,64,128]{4,3,2,0,1:T(8,128)(2,1)S(1)}, u32[]{:S(2)}, u32[]{:S(2)}) collective-permute-start(bf16[4,1,2,64,128]{4,3,2,0,1:T(8,128)(2,1)S(1)} %bitcast.95), channel_id=1, source_target_pairs={{0,1},{1,0},{2,3},{3,2},{4,5},{5,4},{6,7},{7,6},{8,9},{9,8},{10,11... | collective-permute-start | bytes 393224 | tf_op jit(solution)/shard_map/ppermute | solution.py:173
  58.4 8.4 %collective-permute-start.8 = (bf16[4,1,2,64,128]{4,3,2,0,1:T(8,128)(2,1)S(1)}, bf16[4,1,2,64,128]{4,3,2,0,1:T(8,128)(2,1)S(1)}, u32[]{:S(2)}, u32[]{:S(2)}) collective-permute-start(bf16[4,1,2,64,128]{4,3,2,0,1:T(8,128)(2,1)S(1)} %bitcast.94), channel_id=1, source_target_pairs={{0,2},{1,3},{2,0},{3,1},{4,6},{5,7},{6,4},{7,5},{8,10},{9,11},{10,... | collective-permute-start | bytes 393224 | tf_op jit(solution)/shard_map/ppermute | solution.py:173
  60.7 9.3 %collective-permute-start.9 = (bf16[4,1,2,64,128]{4,3,2,0,1:T(8,128)(2,1)S(1)}, bf16[4,1,2,64,128]{4,3,2,0,1:T(8,128)(2,1)S(1)}, u32[]{:S(2)}, u32[]{:S(2)}) collective-permute-start(bf16[4,1,2,64,128]{4,3,2,0,1:T(8,128)(2,1)S(1)} %bitcast.93), channel_id=1, source_target_pairs={{0,3},{1,2},{2,1},{3,0},{4,7},{5,6},{6,5},{7,4},{8,11},{9,10},{10,... | collective-permute-start | bytes 393224 | tf_op jit(solution)/shard_map/ppermute | solution.py:173
  70.1 8.4 %collective-permute-start.10 = (bf16[2,2,64,128]{3,2,1,0:T(8,128)(2,1)S(1)}, bf16[2,2,64,128]{3,2,1,0:T(8,128)(2,1)S(1)}, u32[]{:S(2)}, u32[]{:S(2)}) collective-permute-start(bf16[2,2,64,128]{3,2,1,0:T(8,128)(2,1)S(1)} %get-tuple-element.47), channel_id=1, source_target_pairs={{0,24},{8,16},{16,8},{24,0},{1,25},{9,17},{17,9},{25,1},{2,26},{10... | collective-permute-start | bytes 196616 | tf_op jit(solution)/shard_map/ppermute | solution.py:173
  73.6 13.2 %collective-permute-start.11 = (bf16[2,2,64,128]{3,2,1,0:T(8,128)(2,1)S(1)}, bf16[2,2,64,128]{3,2,1,0:T(8,128)(2,1)S(1)}, u32[]{:S(2)}, u32[]{:S(2)}) collective-permute-start(bf16[2,2,64,128]{3,2,1,0:T(8,128)(2,1)S(1)} %get-tuple-element.48), channel_id=1, source_target_pairs={{0,16},{8,24},{16,0},{24,8},{1,17},{9,25},{17,1},{25,9},{2,18},{10... | collective-permute-start | bytes 196616 | tf_op jit(solution)/shard_map/ppermute | solution.py:173
  73.6 13.2 %collective-permute-start.12 = (bf16[2,2,64,128]{3,2,1,0:T(8,128)(2,1)S(1)}, bf16[2,2,64,128]{3,2,1,0:T(8,128)(2,1)S(1)}, u32[]{:S(2)}, u32[]{:S(2)}) collective-permute-start(bf16[2,2,64,128]{3,2,1,0:T(8,128)(2,1)S(1)} %get-tuple-element.46), channel_id=1, source_target_pairs={{0,8},{8,0},{16,24},{24,16},{1,9},{9,1},{17,25},{25,17},{2,10},{10... | collective-permute-start | bytes 196616 | tf_op jit(solution)/shard_map/ppermute | solution.py:173

commit v2 on v1

v2 whole, which is shorter than its diff:
```python
import functools
import math

import jax
import jax.numpy as jnp
from jax import lax
from jax.experimental import pallas as pl
from jax.experimental.pallas import tpu as pltpu
from jax.sharding import PartitionSpec as P


F32 = jnp.float32
BF16 = jnp.bfloat16
NT = (((1,), (1,)), ((), ()))
NN = (((1,), (0,)), ((), ()))
MASKED = -1e30
VMEM = pl.BlockSpec(memory_space=pltpu.VMEM)
SMEM = pl.BlockSpec(memory_space=pltpu.SMEM)


def dot(a, b, dims):
    return lax.dot_general(a, b, dims, preferred_element_type=F32)


def causal_tile(rows):
    shape = (rows, rows)
    return lax.broadcasted_iota(jnp.int32, shape, 0) <= lax.broadcasted_iota(jnp.int32, shape, 1)


def over_visible(place, tile):
    tile(place, True)

    def turn(k, _):
        tile(k, False)
        return 0

    lax.fori_loop(0, place, turn, 0)


def grad_kernel(group, chunk, scale, slot, slots, inner, zs, table, *refs):
    q_ref, do_ref, delta_ref, kv_ref = refs[:4]
    first, last = slot == 0, slot == slots - 1
    start_refs, refs = ((), refs[4:]) if first else (refs[4:6], refs[6:])
    dq_refs, out_refs = refs[:zs], refs[zs:-10]
    kt_ref, x_ref, m_ref, l_ref, dqt_ref, dka_ref, dva_ref, p_ref, ds_ref, turned_ref = refs[-10:]
    heads, rows, width = q_ref.shape
    blocks = kv_ref.shape[0]
    slice_rows = rows // zs
    scale2 = scale * math.log2(math.e)
    causal = causal_tile(rows)
    core, place_in, z_in = (table[blocks + slots + index] for index in range(3))
    for acc_ref, index in ((dka_ref, 0), (dva_ref, 1)):
        acc_ref[...] = jnp.zeros_like(acc_ref) if first else start_refs[index][...]
    for b in range(blocks):
        kt_ref[b] = kv_ref[b, 0].T
    place = table[blocks + slot]
    for g in range(0, heads, group):

        def totals(k, diag):
            keys = kv_ref[table[k], 0]
            for j in range(group):
                x = dot(keys, q_ref[g + j], NT) * scale2
                if diag:
                    x = jnp.where(causal, x, MASKED)
                x_ref[k, j] = x
                x = x.reshape(rows // 8, 8, rows)
                m_new = jnp.max(x, axis=0)
                if not diag:
                    m_old = m_ref[j]
                    m_new = jnp.maximum(m_old, m_new)
                total = jnp.sum(jnp.exp2(x - m_new[None]), axis=0)
                if not diag:
                    total = total + l_ref[j] * jnp.exp2(m_old - m_new)
                m_ref[j] = m_new
                l_ref[j] = total

        over_visible(place, totals)
        for j in range(group):
            m = m_ref[j]
            high = jnp.max(m, axis=0, keepdims=True)
            total = jnp.sum(l_ref[j] * jnp.exp2(m - high), axis=0, keepdims=True)
            m_ref[j] = jnp.broadcast_to(high + jnp.log2(total), (8, rows))

        def tile(k, diag):
            block = table[k]
            for j in range(group):
                lse_row, delta_row = m_ref[j, 0:1], delta_ref[g + j : g + j + 1, :]
                head = slice(j * rows, (j + 1) * rows)
                for c in range(0, rows, chunk):
                    cut = slice(c, c + chunk)
                    dp = dot(kv_ref[block, 1, cut], do_ref[g + j], NT)
                    p = jnp.exp2(x_ref[k, j, cut] - lse_row)
                    p_ref[cut, head] = p.astype(BF16)
                    ds_ref[cut, head] = (p * (dp - delta_row)).astype(BF16)
            keys_t = kt_ref[block]
            for j in range(group):
                part = dot(keys_t, ds_ref[:, j * rows : (j + 1) * rows], NN)
                if diag:
                    dqt_ref[j] = part
                else:
                    dqt_ref[j] += part
            wide = slice(g, g + group)
            dva_ref[block] += dot(p_ref[...], do_ref[wide].reshape(group * rows, width), NN)
            dka_ref[block] += dot(ds_ref[...], q_ref[wide].reshape(group * rows, width), NN)

        over_visible(place, tile)
        for j in range(group):
            turned_ref[...] = (dqt_ref[j] * scale).T
            for z in range(zs):
                start = pl.multiple_of(partner(z_in, z, zs) * slice_rows, slice_rows)
                dq_refs[z][g + j] = turned_ref[pl.ds(start, slice_rows)].astype(BF16)
    if not last:
        out_refs[0][...] = dka_ref[...]
        out_refs[1][...] = dva_ref[...]
        return
    for step, out_ref in enumerate(out_refs):
        block = partner(core, step // inner, slots) * inner + partner(place_in, step % inner, inner)
        for z in range(zs):
            start = pl.multiple_of(partner(z_in, z, zs) * slice_rows, slice_rows)
            cut = pl.ds(start, slice_rows)
            out_ref[z, 0] = (dka_ref[block, cut] * scale).astype(BF16)
            out_ref[z, 1] = dva_ref[block, cut].astype(BF16)


def grad_call(table, q, do, delta, kv, sums, group, scale, slot, slots, inner, zs):
    heads, rows, width = q.shape
    blocks = kv.shape[0]
    slice_rows = rows // zs
    flops = 5 * heads * rows * rows * blocks * width
    total = (blocks, rows, width)
    outs = [jax.ShapeDtypeStruct((heads, slice_rows, width), BF16)] * zs
    if slot < slots - 1:
        outs += [jax.ShapeDtypeStruct(total, F32)] * 2
    else:
        outs += [jax.ShapeDtypeStruct((zs, 2, slice_rows, width), BF16)] * blocks
    out = pl.pallas_call(
        functools.partial(grad_kernel, group, rows // 2, scale, slot, slots, inner, zs),
        out_shape=outs,
        in_specs=[SMEM] + [VMEM] * (4 + len(sums)),
        out_specs=[VMEM] * len(outs),
        scratch_shapes=[
            pltpu.VMEM((blocks, width, rows), BF16),
            pltpu.VMEM((blocks, group, rows, rows), F32),
            pltpu.VMEM((group, 8, rows), F32),
            pltpu.VMEM((group, 8, rows), F32),
            pltpu.VMEM((group, width, rows), F32),
            pltpu.VMEM(total, F32),
            pltpu.VMEM(total, F32),
            pltpu.VMEM((rows, group * rows), BF16),
            pltpu.VMEM((rows, group * rows), BF16),
            pltpu.VMEM((rows, width), F32),
        ],
        cost_estimate=pl.CostEstimate(flops=flops, bytes_accessed=q.size * 12, transcendentals=0),
    )(table, q, do, delta, kv, *sums)
    return out[:zs], out[zs:]


def exchange(x, axes):
    return lax.all_to_all(x, axes, split_axis=0, concat_axis=0, tiled=True)


def partner(index, step, count):
    if count & (count - 1) == 0:
        return index ^ step
    return (step - index) % count


def trade(x, axes, steps):
    counts = [lax.axis_size(axis) for axis in axes]
    pairs = []
    for device in range(math.prod(counts)):
        target, rest = 0, device
        places = []
        for count in reversed(counts):
            places.insert(0, rest % count)
            rest //= count
        for spot, step, count in zip(places, steps, counts):
            target = target * count + partner(spot, step, count)
        pairs.append((device, target))
    return lax.ppermute(x, axes, pairs)


def natural(pieces, index):
    count = len(pieces)

    def pick(place):
        kept = pieces[0]
        for step in range(1, count):
            kept = jnp.where(partner(index, step, count) == place, pieces[step], kept)
        return kept

    return [pick(place) for place in range(count)]


def body(query, keys, values, forward_output, d_out, span_order):
    rows, heads, width = query.shape
    kv_count = keys.shape[1]
    scale = width ** (-0.5)
    cores, inner, zs = lax.axis_size("outer"), lax.axis_size("inner"), lax.axis_size("head")
    core, place, z_in = (lax.axis_index(axis) for axis in ("outer", "inner", "head"))
    blocks = cores * inner
    own_heads = heads // cores
    shared = kv_count % cores != 0
    own_kv = 1 if shared else kv_count // cores
    group_heads = own_heads // own_kv
    slice_rows = rows // zs
    group = max(1, min(8, group_heads, 64 // blocks))

    kv = jnp.stack([jnp.moveaxis(keys, 1, 0), jnp.moveaxis(values, 1, 0)], axis=1)
    kv = jnp.broadcast_to(kv, (cores,) + kv.shape) if shared else kv.reshape((cores, own_kv) + kv.shape[1:])
    kv = jnp.broadcast_to(kv[:, None], (cores, inner) + kv.shape[1:])
    kv = exchange(kv.reshape((blocks,) + kv.shape[2:]), ("outer", "inner"))

    def share(x):
        x = jnp.moveaxis(x, 1, 0)
        x = x.reshape((cores, own_heads) + x.shape[1:])
        got = [lax.dynamic_index_in_dim(x, core, 0, keepdims=False)]
        for step in range(1, cores):
            away = lax.dynamic_index_in_dim(x, partner(core, step, cores), 0, keepdims=False)
            got.append(trade(away, ("outer",), (step,)))
        return got

    delta = jnp.sum(d_out.astype(F32) * forward_output.astype(F32), axis=-1)
    q_all, do_all, delta_all = share(query), share(d_out), share(delta)

    order = span_order[0]
    ids = jnp.arange(blocks, dtype=jnp.int32)
    by_place = jnp.sum(jnp.where(order[None, :] == ids[:, None], ids[None, :], 0), axis=1)
    own_blocks = jnp.stack([partner(core, step, cores) for step in range(cores)]) * inner + place
    places = jnp.sum(jnp.where(own_blocks[:, None] == ids[None, :], order[None, :], 0), axis=1)
    table = jnp.concatenate([by_place, places, jnp.stack([core, place, z_in]).astype(jnp.int32)])

    sums = [()] * own_kv
    dq = []
    for slot in range(cores):
        parts = []
        for g in range(own_kv):
            mine = slice(g * group_heads, (g + 1) * group_heads)
            operands = (x[slot][mine] for x in (q_all, do_all, delta_all))
            part, sums[g] = grad_call(
                table, *operands, kv[:, g], sums[g], group, scale, slot, cores, inner, zs
            )
            parts.append(part)
        parts = [jnp.concatenate(part, axis=0) for part in zip(*parts)]
        got = []
        for z in range(zs):
            got.append(trade(parts[z], ("head", "outer"), (z, slot)) if z or slot else parts[z])
        dq.append(jnp.stack(natural(got, z_in)))
    dq = jnp.stack(natural(dq, core), axis=1)
    dq = jnp.transpose(dq, (3, 0, 1, 2, 4)).reshape(1, slice_rows, zs * heads, width)
    pieces = [jnp.stack(part, axis=1) for part in zip(*sums)]

    sums = [None] * cores
    for step, part in enumerate(pieces):
        c, i = divmod(step, inner)
        if step:
            part = trade(part, ("outer", "inner"), (c, i))
        part = part.astype(F32)
        sums[c] = part if sums[c] is None else sums[c] + part
    if shared:
        sums = [sum(sums)]
    else:
        sums = natural(sums, core)
    sums = jnp.concatenate(sums, axis=1).astype(BF16)

    got = [sums[0]]
    for z in range(1, zs):
        got.append(trade(sums[z], ("head",), (z,)))
    sums = jnp.stack(natural(got, z_in))
    sums = jnp.transpose(sums, (2, 3, 0, 1, 4)).reshape(2, 1, slice_rows, zs * kv_count, width)
    return dq, sums[0], sums[1]


def solution(mesh):
    rows_spec = P(("outer", "inner"), "head", None)
    out_spec = P(("outer", "inner"), "head", None, None)
    return jax.shard_map(
        body,
        mesh=mesh,
        in_specs=(rows_spec,) * 5 + (P(),),
        out_specs=(out_spec,) * 3,
        check_vma=False,
    )
```

time: 90.4 us -> 98 us (1.084); the launches traced: 90.1 us -> 96.5 us
  starting transfers between devices: 22 us -> 29.4 us
  waiting for transfers between devices: 29.4 us -> 23.5 us
  Pallas kernels: 25.6 us -> 29.9 us
  other arithmetic: 2.58 us -> 3.92 us
    ppermute x10 -> x20, starting transfers between devices: 10.2 us -> 24 us  [trade(): return lax.ppermute(x, axes, pairs)]
    ppermute x10 -> x20, waiting for transfers between devices: 21.8 us -> 14.8 us  [trade(): return lax.ppermute(x, axes, pairs)]
    all_to_all x2 -> x1, starting transfers between devices: 10.8 us -> 5.33 us  [exchange(): return lax.all_to_all(x, axes, split_axis=0, concat_axis=0, tiled=True)]
    pallas_call x1 -> x2, Pallas kernels: 25.6 us -> 29.9 us  [grad_call(): pl.pallas_call(functools.partial(grad_kernel, group, rows // 2, scale, sl...]
    transpose x1 -> x0, local copies, waits for them, and re-layouts: 1.65 us -> none  [body(): jnp.transpose(dq, (3, 1, 0, 2, 4)).reshape(1, slice_rows, zs * heads, width)]
    another operation x1 -> x4, other arithmetic: 0.18 us -> 1.31 us
    all_to_all x2 -> x1, waiting for transfers between devices: 7.59 us -> 8.63 us  [exchange(): return lax.all_to_all(x, axes, split_axis=0, concat_axis=0, tiled=True)]
    ppermute x3 -> x0, starting transfers between devices: 1.01 us -> none  [share(): lax.ppermute(out, 'outer', [(d, (d + step) % cores) for d in range(cores)])]
  transfers between devices with their start and end apart: 15 -> 21, of which waited for: 7 -> 7; matrix products, arithmetic and copies ran while one was open for 9% -> 8% of each run, Pallas kernels for 0% -> 14%
where the time goes in v2:
time: 98 us; the launch traced here: 96.5 us
  Pallas kernels  29.9 us (31%)
  starting transfers between devices  29.4 us (30%)
  waiting for transfers between devices  23.5 us (24%)
  local copies, waits for them, and re-layouts  8.99 us (9%)
  other arithmetic  3.92 us (4%)
    pallas_call x2, Pallas kernels, grad_call(): pl.pallas_call(functools.partial(grad_kernel, group, rows // 2, scale, sl...  29.9 us
    ppermute x20, starting transfers between devices, trade(): return lax.ppermute(x, axes, pairs)  24 us
    ppermute x20, waiting for transfers between devices, trade(): return lax.ppermute(x, axes, pairs)  14.8 us
    all_to_all x1, waiting for transfers between devices, exchange(): return lax.all_to_all(x, axes, split_axis=0, concat_axis=0, tiled=True)  8.63 us
    unnamed x25, local copies, waits for them, and re-layouts  6.06 us
    all_to_all x1, starting transfers between devices, exchange(): return lax.all_to_all(x, axes, split_axis=0, concat_axis=0, tiled=True)  5.33 us
  transfers between devices with their start and end apart: 21, of which 7 were waited for; matrix products, arithmetic and copies ran while one was open for 8% of the time, Pallas kernels for 14%

profile of v2, /device:TPU:0, one launch (start us, length us, event | category | flops | bytes accessed | tf_op | source)
XLA Modules:
  0.0 96.5 jit_solution(12972830130083521475)
XLA Ops:
  0.6 1.4 %pad_maximum_fusion.3 = bf16[2,2,256,128]{3,0,2,1:T(2,128)(2,1)S(1)} fusion(bf16[2,1,256,128]{3,0,2,1:T(2,128)(2,1)} %bitcast.107, bf16[2,1,256,128]{3,0,2,1:T(2,128)(2,1)} %bitcast.108), kind=kLoop, calls=%fused_computation.16 | loop fusion | flops 131072 | bytes 524288 | tf_op jit(solution)/shard_map/stack | solution.py:209
  2.0 1.2 %broadcast_in_dim.39 = bf16[2,4,2,256,128]{4,3,2,1,0:T(8,128)(2,1)} broadcast(bf16[2,2,256,128]{3,2,1,0:T(8,128)(2,1)S(1)} %copy.48), dimensions={0,2,3,4} | broadcast | bytes 1310720 | tf_op jit(solution)/shard_map/broadcast_in_dim | solution.py:211
  3.2 5.3 %all-to-all-start = ((bf16[8,1,2,256,128]{4,3,2,1,0:T(8,128)(2,1)}), bf16[8,1,2,256,128]{4,3,2,1,0:T(8,128)(2,1)}, u32[]{:S(2)}, u32[]{:S(2)}) async-start(bf16[8,1,2,256,128]{4,3,2,1,0:T(8,128)(2,1)} %bitcast.18), calls=%async_computation | async-start | bytes 2097152 | tf_op jit(solution)/shard_map/all_to_all | solution.py:159
  8.6 0.4 constant_dynamic-slice_fusion.2
  8.9 0.0 copy-start.2
  8.9 0.1 copy.71
  9.0 0.6 collective-permute-start
  9.6 0.1 copy.70
  9.7 0.1 collective-permute-start.1
  9.8 0.4 copy-done.2
  10.2 0.6 multiply_reduce_fusion
  10.8 0.1 copy.47
  10.9 0.6 dynamic-slice_bitcast_fusion.1
  11.5 0.5 collective-permute-start.2
  12.0 0.1 fusion.10
  12.0 0.9 copy.68
  12.9 0.9 copy.69
  13.8 0.1 select_reduce_fusion
  13.9 0.2 fusion.9
  14.1 0.7 concatenate.39.table
  14.8 8.6 %all-to-all-done = bf16[8,1,2,256,128]{4,3,2,1,0:T(8,128)(2,1)} async-done(((bf16[8,1,2,256,128]{4,3,2,1,0:T(8,128)(2,1)}), bf16[8,1,2,256,128]{4,3,2,1,0:T(8,128)(2,1)}, u32[]{:S(2)}, u32[]{:S(2)}) %all-to-all-start) | async-done | bytes 1048608 | tf_op jit(solution)/shard_map/all_to_all | solution.py:159
  23.4 13.7 %shard_map.85 = (bf16[8,64,128]{2,1,0:T(8,128)(2,1)}, bf16[8,64,128]{2,1,0:T(8,128)(2,1)}, bf16[8,64,128]{2,1,0:T(8,128)(2,1)}, bf16[8,64,128]{2,1,0:T(8,128)(2,...) custom-call(s32[13]{0:T(128)} %concatenate.39.table, bf16[8,256,128]{2,1,0:T(8,128)(2,1)} %bitcast.104, ...), custom_call_target="tpu_custom_call" | custom-call | flops 2684354560 | bytes 3145728 | tf_op jit(solution)/shard_map/pallas_call | solution.py:136
  37.1 0.0 collective-permute-done.2.refs_2_
  37.1 0.0 collective-permute-done.refs_0_
  37.1 0.0 collective-permute-done.1.refs_1_
  37.1 0.6 copy-done.7
  37.7 16.2 %shard_map.86 = (bf16[8,64,128]{2,1,0:T(8,128)(2,1)}, bf16[8,64,128]{2,1,0:T(8,128)(2,1)}, bf16[8,64,128]{2,1,0:T(8,128)(2,1)}, bf16[8,64,128]{2,1,0:T(8,128)(2,...) custom-call(s32[13]{0:T(128)} %concatenate.39.table, ...), custom_call_target="tpu_custom_call" | custom-call | flops 2684354560 | bytes 3145728 | tf_op jit(solution)/shard_map/pallas_call | solution.py:136
  53.9 0.5 collective-permute-start.10
  54.4 0.0 collective-permute-start.11
  54.4 0.9 collective-permute-start.12
  55.3 2.1 %collective-permute-start.13 = (bf16[4,1,2,64,128]{4,3,2,0,1:T(8,128)(2,1)}, bf16[4,1,2,64,128]{4,3,2,0,1:T(8,128)(2,1)S(1)}, u32[]{:S(2)}, u32[]{:S(2)}) collective-permute-start(bf16[4,1,2,64,128]{4,3,2,0,1:T(8,128)(2,1)} %bitcast.113), channel_id=1, source_target_pairs={{0,7},{1,6},{2,5},{3,4},{4,3},{5,2},{6,1},{7,0},{8,15},{9,14},{10,... | collective-permute-start | bytes 393224 | tf_op jit(solution)/shard_map/ppermute | solution.py:180
  57.3 0.3 collective-permute-start.14
  57.6 0.0 collective-permute-done.10
  57.6 0.9 collective-permute-start.15
  58.5 1.6 %collective-permute-done.11 = bf16[4,1,2,64,128]{4,3,2,0,1:T(8,128)(2,1)S(1)} collective-permute-done((bf16[4,1,2,64,128]{4,3,2,0,1:T(8,128)(2,1)}, bf16[4,1,2,64,128]{4,3,2,0,1:T(8,128)(2,1)S(1)}, u32[]{:S(2)}, u32[]{:S(2)}) %collective-permute-start.11) | collective-permute-done | bytes 131104 | tf_op jit(solution)/shard_map/ppermute | solution.py:180
  60.1 0.8 collective-permute-start.16
  60.9 3.8 %collective-permute-start.3 = (bf16[8,64,128]{2,1,0:T(8,128)(2,1)}, bf16[8,64,128]{2,1,0:T(8,128)(2,1)S(1)}, u32[]{:S(2)}, u32[]{:S(2)}) collective-permute-start(bf16[8,64,128]{2,1,0:T(8,128)(2,1)} %get-tuple-element.23), channel_id=1, source_target_pairs={{0,28},{4,24},{8,20},{12,16},{16,12},{20,8},{24,4},{28,0},{1,29},{... | collective-permute-start | bytes 393224 | tf_op jit(solution)/shard_map/ppermute | solution.py:180
  64.8 0.0 collective-permute-done.13
  64.8 1.8 %collective-permute-start.4 = (bf16[8,64,128]{2,1,0:T(8,128)(2,1)}, bf16[8,64,128]{2,1,0:T(8,128)(2,1)S(1)}, u32[]{:S(2)}, u32[]{:S(2)}) collective-permute-start(bf16[8,64,128]{2,1,0:T(8,128)(2,1)} %get-tuple-element.24), channel_id=1, source_target_pairs={{0,20},{4,16},{8,28},{12,24},{16,4},{20,0},{24,12},{28,8},{1,21},{... | collective-permute-start | bytes 393224 | tf_op jit(solution)/shard_map/ppermute | solution.py:180
  66.6 0.0 collective-permute-done.14
  66.6 0.9 collective-permute-start.5
  67.5 0.0 collective-permute-done.15
  67.5 1.0 %collective-permute-start.6 = (bf16[8,64,128]{2,1,0:T(8,128)(2,1)}, bf16[8,64,128]{2,1,0:T(8,128)(2,1)S(1)}, u32[]{:S(2)}, u32[]{:S(2)}) collective-permute-start(bf16[8,64,128]{2,1,0:T(8,128)(2,1)} %get-tuple-element.26), channel_id=1, source_target_pairs={{0,4},{4,0},{8,12},{12,8},{16,20},{20,16},{24,28},{28,24},{1,5},{5... | collective-permute-start | bytes 393224 | tf_op jit(solution)/shard_map/ppermute | solution.py:180
  68.5 0.6 collective-permute-done.16
  69.2 4.0 %collective-permute-start.7 = (bf16[8,64,128]{2,1,0:T(8,128)(2,1)S(1)}, bf16[8,64,128]{2,1,0:T(8,128)(2,1)S(1)}, u32[]{:S(2)}, u32[]{:S(2)}) collective-permute-start(bf16[8,64,128]{2,1,0:T(8,128)(2,1)S(1)} %copy-done.6), channel_id=1, source_target_pairs={{0,24},{4,28},{8,16},{12,20},{16,8},{20,12},{24,0},{28,4},{1,25},{... | collective-permute-start | bytes 393224 | tf_op jit(solution)/shard_map/ppermute | solution.py:180
  73.2 1.1 %select_convert_fusion = (bf16[4,1,2,64,128]{4,3,2,0,1:T(8,128)(2,1)S(1)}, bf16[4,1,2,64,128]{4,3,2,0,1:T(8,128)(2,1)S(1)}) fusion(pred[]{:T(512)S(6)} %eq.116, bf16[4,1,2,64,128]{4,3,2,0,1:T(8,128)(2,1)S(1)} %collective-permute-done.13, bf16[4,1,2,64,128]{4,3,2,0,1:T(8,128)(2,1)S(1)} %collective-permute-done.12, ...), kind=kLoop, calls=%fused_computation.21 | loop fusion | flops 1179648 | bytes 1310722 | tf_op jit(solution)/shard_map/convert.2
  74.3 0.0 copy-start.3
  74.3 0.8 collective-permute-start.8
  75.1 6.9 %collective-permute-done.4 = bf16[8,64,128]{2,1,0:T(8,128)(2,1)S(1)} collective-permute-done((bf16[8,64,128]{2,1,0:T(8,128)(2,1)}, bf16[8,64,128]{2,1,0:T(8,128)(2,1)S(1)}, u32[]{:S(2)}, u32[]{:S(2)}) %collective-permute-start.4) | collective-permute-done | bytes 131104 | tf_op jit(solution)/shard_map/ppermute | solution.py:180
  82.0 0.6 collective-permute-start.9
  82.6 1.9 %collective-permute-start.17 = (bf16[2,2,64,128]{3,2,1,0:T(8,128)(2,1)S(1)}, bf16[2,2,64,128]{3,2,1,0:T(8,128)(2,1)S(1)}, u32[]{:S(2)}, u32[]{:S(2)}) collective-permute-start(bf16[2,2,64,128]{3,2,1,0:T(8,128)(2,1)S(1)} %get-tuple-element.75), channel_id=1, source_target_pairs={{0,24},{8,16},{16,8},{24,0},{1,25},{9,17},{17,9},{25,1},{2,26},{10... | collective-permute-start | bytes 196616 | tf_op jit(solution)/shard_map/ppermute | solution.py:180
  84.5 1.0 collective-permute-start.18
  85.5 0.1 select_bitcast_fusion.7
  85.6 1.6 %collective-permute-start.19 = (bf16[2,2,64,128]{3,2,1,0:T(8,128)(2,1)S(1)}, bf16[2,2,64,128]{3,2,1,0:T(8,128)(2,1)S(1)}, u32[]{:S(2)}, u32[]{:S(2)}) collective-permute-start(bf16[2,2,64,128]{3,2,1,0:T(8,128)(2,1)S(1)} %get-tuple-element.74), channel_id=1, source_target_pairs={{0,8},{8,0},{16,24},{24,16},{1,9},{9,1},{17,25},{25,17},{2,10},{10... | collective-permute-start | bytes 196616 | tf_op jit(solution)/shard_map/ppermute | solution.py:180
  87.2 1.4 %collective-permute-done.8 = bf16[8,64,128]{2,1,0:T(8,128)(2,1)S(1)} collective-permute-done((bf16[8,64,128]{2,1,0:T(8,128)(2,1)S(1)}, bf16[8,64,128]{2,1,0:T(8,128)(2,1)S(1)}, u32[]{:S(2)}, u32[]{:S(2)}) %collective-permute-start.8) | collective-permute-done | bytes 131104 | tf_op jit(solution)/shard_map/ppermute | solution.py:180
  88.5 4.0 %collective-permute-done.9 = bf16[8,64,128]{2,1,0:T(8,128)(2,1)S(1)} collective-permute-done((bf16[8,64,128]{2,1,0:T(8,128)(2,1)S(1)}, bf16[8,64,128]{2,1,0:T(8,128)(2,1)S(1)}, u32[]{:S(2)}, u32[]{:S(2)}) %collective-permute-start.9) | collective-permute-done | bytes 131104 | tf_op jit(solution)/shard_map/ppermute | solution.py:180
  92.5 0.1 select_bitcast_fusion.3
  92.6 0.1 broadcast_select_fusion.1
  92.8 0.1 pad_maximum_fusion
  92.9 1.6 %copy.54 = bf16[1,64,64,128]{3,2,1,0:T(8,128)(2,1)} copy(bf16[1,64,64,128]{3,1,2,0:T(8,128)(2,1)S(1)} %bitcast.98) | data formatting | bytes 2097152
  94.5 0.0 collective-permute-done.18
  94.5 0.3 collective-permute-done.19
  95.0 0.7 copy.55
  95.8 0.7 copy.56
  (26 shorter events, 0.2 us)
Async XLA Ops:
  3.2 5.3 %copy-start = (bf16[256,16,128]{2,1,0:T(8,128)(2,1)S(1)}, bf16[256,16,128]{2,1,0:T(8,128)(2,1)}, u32[]{:S(2)}) copy-start(bf16[256,16,128]{2,1,0:T(8,128)(2,1)} %param.10) | copy-start | bytes 3145732
  3.2 5.3 %copy-start.1 = (bf16[256,16,128]{2,1,0:T(8,128)(2,1)S(1)}, bf16[256,16,128]{2,1,0:T(8,128)(2,1)}, u32[]{:S(2)}) copy-start(bf16[256,16,128]{2,1,0:T(8,128)(2,1)} %param.6) | copy-start | bytes 3145732
  3.2 20.2 %all-to-all-start = ((bf16[8,1,2,256,128]{4,3,2,1,0:T(8,128)(2,1)}), bf16[8,1,2,256,128]{4,3,2,1,0:T(8,128)(2,1)}, u32[]{:S(2)}, u32[]{:S(2)}) async-start(bf16[8,1,2,256,128]{4,3,2,1,0:T(8,128)(2,1)} %bitcast.18), calls=%async_computation | async-start | bytes 2097152 | tf_op jit(solution)/shard_map/all_to_all | solution.py:159
  8.9 1.2 %copy-start.2 = (bf16[256,16,128]{2,1,0:T(8,128)(2,1)S(1)}, bf16[256,16,128]{2,1,0:T(8,128)(2,1)}, u32[]{:S(2)}) copy-start(bf16[256,16,128]{2,1,0:T(8,128)(2,1)} %param.9) | copy-start | bytes 3145732
  9.0 28.1 %collective-permute-start = (bf16[8,256,128]{2,1,0:T(8,128)(2,1)S(1)}, bf16[8,256,128]{2,1,0:T(8,128)(2,1)}, u32[]{:S(2)}, u32[]{:S(2)}) collective-permute-start(bf16[8,256,128]{2,1,0:T(8,128)(2,1)S(1)} %bitcast.101), channel_id=1, source_target_pairs={{0,4},{4,0},{1,5},{5,1},{2,6},{6,2},{3,7},{7,3},{8,12},{12,8},{9,1... | collective-permute-start | bytes 1572872 | tf_op jit(solution)/shard_map/ppermute | solution.py:180
  9.7 27.4 %collective-permute-start.1 = (bf16[8,256,128]{2,1,0:T(8,128)(2,1)S(1)}, bf16[8,256,128]{2,1,0:T(8,128)(2,1)}, u32[]{:S(2)}, u32[]{:S(2)}) collective-permute-start(bf16[8,256,128]{2,1,0:T(8,128)(2,1)S(1)} %bitcast.102), channel_id=1, source_target_pairs={{0,4},{4,0},{1,5},{5,1},{2,6},{6,2},{3,7},{7,3},{8,12},{12,8},{9,1... | collective-permute-start | bytes 1572872 | tf_op jit(solution)/shard_map/ppermute | solution.py:180
  11.5 25.6 %collective-permute-start.2 = (f32[8,256]{1,0:T(8,128)S(1)}, f32[8,256]{1,0:T(8,128)S(1)}, u32[]{:S(2)}, u32[]{:S(2)}) collective-permute-start(f32[8,256]{1,0:T(8,128)S(1)} %get-tuple-element.77), channel_id=1, source_target_pairs={{0,4},{4,0},{1,5},{5,1},{2,6},{6,2},{3,7},{7,3},{8,12},{12,8},{9,1... | collective-permute-start | bytes 24584 | tf_op jit(solution)/shard_map/ppermute | solution.py:180
  12.0 1.8 %copy-start.8 = (s32[1,8]{1,0:T(1,128)S(1)}, s32[1,8]{1,0:T(1,128)}, u32[]{:S(2)}) copy-start(s32[1,8]{1,0:T(1,128)} %param.11) | copy-start | bytes 100
  37.1 0.6 copy-start.7
  37.7 31.5 %copy-start.6 = (bf16[8,64,128]{2,1,0:T(8,128)(2,1)S(1)}, bf16[8,64,128]{2,1,0:T(8,128)(2,1)}, u32[]{:S(2)}) copy-start(bf16[8,64,128]{2,1,0:T(8,128)(2,1)} %get-tuple-element.27) | copy-start | bytes 393220
  53.9 20.4 %copy-start.5 = (bf16[8,64,128]{2,1,0:T(8,128)(2,1)S(1)}, bf16[8,64,128]{2,1,0:T(8,128)(2,1)}, u32[]{:S(2)}) copy-start(bf16[8,64,128]{2,1,0:T(8,128)(2,1)} %get-tuple-element.28) | copy-start | bytes 393220
  53.9 28.1 %copy-start.4 = (bf16[8,64,128]{2,1,0:T(8,128)(2,1)S(1)}, bf16[8,64,128]{2,1,0:T(8,128)(2,1)}, u32[]{:S(2)}) copy-start(bf16[8,64,128]{2,1,0:T(8,128)(2,1)} %get-tuple-element.29) | copy-start | bytes 393220
  53.9 3.7 %collective-permute-start.10 = (bf16[4,1,2,64,128]{4,3,2,0,1:T(8,128)(2,1)}, bf16[4,1,2,64,128]{4,3,2,0,1:T(8,128)(2,1)S(1)}, u32[]{:S(2)}, u32[]{:S(2)}) collective-permute-start(bf16[4,1,2,64,128]{4,3,2,0,1:T(8,128)(2,1)} %bitcast.116), channel_id=1, source_target_pairs={{0,4},{1,5},{2,6},{3,7},{4,0},{5,1},{6,2},{7,3},{8,12},{9,13},{10,... | collective-permute-start | bytes 393224 | tf_op jit(solution)/shard_map/ppermute | solution.py:180
  54.4 5.7 %collective-permute-start.11 = (bf16[4,1,2,64,128]{4,3,2,0,1:T(8,128)(2,1)}, bf16[4,1,2,64,128]{4,3,2,0,1:T(8,128)(2,1)S(1)}, u32[]{:S(2)}, u32[]{:S(2)}) collective-permute-start(bf16[4,1,2,64,128]{4,3,2,0,1:T(8,128)(2,1)} %bitcast.115), channel_id=1, source_target_pairs={{0,5},{1,4},{2,7},{3,6},{4,1},{5,0},{6,3},{7,2},{8,13},{9,12},{10,... | collective-permute-start | bytes 393224 | tf_op jit(solution)/shard_map/ppermute | solution.py:180
  54.4 6.5 %collective-permute-start.12 = (bf16[4,1,2,64,128]{4,3,2,0,1:T(8,128)(2,1)}, bf16[4,1,2,64,128]{4,3,2,0,1:T(8,128)(2,1)S(1)}, u32[]{:S(2)}, u32[]{:S(2)}) collective-permute-start(bf16[4,1,2,64,128]{4,3,2,0,1:T(8,128)(2,1)} %bitcast.114), channel_id=1, source_target_pairs={{0,6},{1,7},{2,4},{3,5},{4,2},{5,3},{6,0},{7,1},{8,14},{9,15},{10,... | collective-permute-start | bytes 393224 | tf_op jit(solution)/shard_map/ppermute | solution.py:180
  55.3 9.5 %collective-permute-start.13 = (bf16[4,1,2,64,128]{4,3,2,0,1:T(8,128)(2,1)}, bf16[4,1,2,64,128]{4,3,2,0,1:T(8,128)(2,1)S(1)}, u32[]{:S(2)}, u32[]{:S(2)}) collective-permute-start(bf16[4,1,2,64,128]{4,3,2,0,1:T(8,128)(2,1)} %bitcast.113), channel_id=1, source_target_pairs={{0,7},{1,6},{2,5},{3,4},{4,3},{5,2},{6,1},{7,0},{8,15},{9,14},{10,... | collective-permute-start | bytes 393224 | tf_op jit(solution)/shard_map/ppermute | solution.py:180
  57.3 9.2 %collective-permute-start.14 = (bf16[4,1,2,64,128]{4,3,2,0,1:T(8,128)(2,1)}, bf16[4,1,2,64,128]{4,3,2,0,1:T(8,128)(2,1)S(1)}, u32[]{:S(2)}, u32[]{:S(2)}) collective-permute-start(bf16[4,1,2,64,128]{4,3,2,0,1:T(8,128)(2,1)} %bitcast.112), channel_id=1, source_target_pairs={{0,1},{1,0},{2,3},{3,2},{4,5},{5,4},{6,7},{7,6},{8,9},{9,8},{10,11... | collective-permute-start | bytes 393224 | tf_op jit(solution)/shard_map/ppermute | solution.py:180
  57.6 9.9 %collective-permute-start.15 = (bf16[4,1,2,64,128]{4,3,2,0,1:T(8,128)(2,1)}, bf16[4,1,2,64,128]{4,3,2,0,1:T(8,128)(2,1)S(1)}, u32[]{:S(2)}, u32[]{:S(2)}) collective-permute-start(bf16[4,1,2,64,128]{4,3,2,0,1:T(8,128)(2,1)} %bitcast.111), channel_id=1, source_target_pairs={{0,2},{1,3},{2,0},{3,1},{4,6},{5,7},{6,4},{7,5},{8,10},{9,11},{10,... | collective-permute-start | bytes 393224 | tf_op jit(solution)/shard_map/ppermute | solution.py:180
  60.1 9.0 %collective-permute-start.16 = (bf16[4,1,2,64,128]{4,3,2,0,1:T(8,128)(2,1)}, bf16[4,1,2,64,128]{4,3,2,0,1:T(8,128)(2,1)S(1)}, u32[]{:S(2)}, u32[]{:S(2)}) collective-permute-start(bf16[4,1,2,64,128]{4,3,2,0,1:T(8,128)(2,1)} %bitcast.110), channel_id=1, source_target_pairs={{0,3},{1,2},{2,1},{3,0},{4,7},{5,6},{6,5},{7,4},{8,11},{9,10},{10,... | collective-permute-start | bytes 393224 | tf_op jit(solution)/shard_map/ppermute | solution.py:180
  60.9 13.4 %collective-permute-start.3 = (bf16[8,64,128]{2,1,0:T(8,128)(2,1)}, bf16[8,64,128]{2,1,0:T(8,128)(2,1)S(1)}, u32[]{:S(2)}, u32[]{:S(2)}) collective-permute-start(bf16[8,64,128]{2,1,0:T(8,128)(2,1)} %get-tuple-element.23), channel_id=1, source_target_pairs={{0,28},{4,24},{8,20},{12,16},{16,12},{20,8},{24,4},{28,0},{1,29},{... | collective-permute-start | bytes 393224 | tf_op jit(solution)/shard_map/ppermute | solution.py:180
  64.8 17.2 %collective-permute-start.4 = (bf16[8,64,128]{2,1,0:T(8,128)(2,1)}, bf16[8,64,128]{2,1,0:T(8,128)(2,1)S(1)}, u32[]{:S(2)}, u32[]{:S(2)}) collective-permute-start(bf16[8,64,128]{2,1,0:T(8,128)(2,1)} %get-tuple-element.24), channel_id=1, source_target_pairs={{0,20},{4,16},{8,28},{12,24},{16,4},{20,0},{24,12},{28,8},{1,21},{... | collective-permute-start | bytes 393224 | tf_op jit(solution)/shard_map/ppermute | solution.py:180
  66.6 16.0 %collective-permute-start.5 = (bf16[8,64,128]{2,1,0:T(8,128)(2,1)}, bf16[8,64,128]{2,1,0:T(8,128)(2,1)S(1)}, u32[]{:S(2)}, u32[]{:S(2)}) collective-permute-start(bf16[8,64,128]{2,1,0:T(8,128)(2,1)} %get-tuple-element.25), channel_id=1, source_target_pairs={{0,12},{4,8},{8,4},{12,0},{16,28},{20,24},{24,20},{28,16},{1,13},{... | collective-permute-start | bytes 393224 | tf_op jit(solution)/shard_map/ppermute | solution.py:180
  67.5 17.0 %collective-permute-start.6 = (bf16[8,64,128]{2,1,0:T(8,128)(2,1)}, bf16[8,64,128]{2,1,0:T(8,128)(2,1)S(1)}, u32[]{:S(2)}, u32[]{:S(2)}) collective-permute-start(bf16[8,64,128]{2,1,0:T(8,128)(2,1)} %get-tuple-element.26), channel_id=1, source_target_pairs={{0,4},{4,0},{8,12},{12,8},{16,20},{20,16},{24,28},{28,24},{1,5},{5... | collective-permute-start | bytes 393224 | tf_op jit(solution)/shard_map/ppermute | solution.py:180
  69.2 16.4 %collective-permute-start.7 = (bf16[8,64,128]{2,1,0:T(8,128)(2,1)S(1)}, bf16[8,64,128]{2,1,0:T(8,128)(2,1)S(1)}, u32[]{:S(2)}, u32[]{:S(2)}) collective-permute-start(bf16[8,64,128]{2,1,0:T(8,128)(2,1)S(1)} %copy-done.6), channel_id=1, source_target_pairs={{0,24},{4,28},{8,16},{12,20},{16,8},{20,12},{24,0},{28,4},{1,25},{... | collective-permute-start | bytes 393224 | tf_op jit(solution)/shard_map/ppermute | solution.py:180
  74.3 18.3 %copy-start.3 = (bf16[8,64,128]{2,1,0:T(8,128)(2,1)S(1)}, bf16[8,64,128]{2,1,0:T(8,128)(2,1)}, u32[]{:S(2)}) copy-start(bf16[8,64,128]{2,1,0:T(8,128)(2,1)} %get-tuple-element.30) | copy-start | bytes 393220
  74.3 14.2 %collective-permute-start.8 = (bf16[8,64,128]{2,1,0:T(8,128)(2,1)S(1)}, bf16[8,64,128]{2,1,0:T(8,128)(2,1)S(1)}, u32[]{:S(2)}, u32[]{:S(2)}) collective-permute-start(bf16[8,64,128]{2,1,0:T(8,128)(2,1)S(1)} %copy-done.5), channel_id=1, source_target_pairs={{0,16},{4,20},{8,24},{12,28},{16,0},{20,4},{24,8},{28,12},{1,17},{... | collective-permute-start | bytes 393224 | tf_op jit(solution)/shard_map/ppermute | solution.py:180
  82.0 10.5 %collective-permute-start.9 = (bf16[8,64,128]{2,1,0:T(8,128)(2,1)S(1)}, bf16[8,64,128]{2,1,0:T(8,128)(2,1)S(1)}, u32[]{:S(2)}, u32[]{:S(2)}) collective-permute-start(bf16[8,64,128]{2,1,0:T(8,128)(2,1)S(1)} %copy-done.4), channel_id=1, source_target_pairs={{0,8},{4,12},{8,0},{12,4},{16,24},{20,28},{24,16},{28,20},{1,9},{5... | collective-permute-start | bytes 393224 | tf_op jit(solution)/shard_map/ppermute | solution.py:180
  82.6 11.9 %collective-permute-start.17 = (bf16[2,2,64,128]{3,2,1,0:T(8,128)(2,1)S(1)}, bf16[2,2,64,128]{3,2,1,0:T(8,128)(2,1)S(1)}, u32[]{:S(2)}, u32[]{:S(2)}) collective-permute-start(bf16[2,2,64,128]{3,2,1,0:T(8,128)(2,1)S(1)} %get-tuple-element.75), channel_id=1, source_target_pairs={{0,24},{8,16},{16,8},{24,0},{1,25},{9,17},{17,9},{25,1},{2,26},{10... | collective-permute-start | bytes 196616 | tf_op jit(solution)/shard_map/ppermute | solution.py:180
  84.5 10.0 %collective-permute-start.18 = (bf16[2,2,64,128]{3,2,1,0:T(8,128)(2,1)S(1)}, bf16[2,2,64,128]{3,2,1,0:T(8,128)(2,1)S(1)}, u32[]{:S(2)}, u32[]{:S(2)}) collective-permute-start(bf16[2,2,64,128]{3,2,1,0:T(8,128)(2,1)S(1)} %get-tuple-element.76), channel_id=1, source_target_pairs={{0,16},{8,24},{16,0},{24,8},{1,17},{9,25},{17,1},{25,9},{2,18},{10... | collective-permute-start | bytes 196616 | tf_op jit(solution)/shard_map/ppermute | solution.py:180
  85.6 9.3 %collective-permute-start.19 = (bf16[2,2,64,128]{3,2,1,0:T(8,128)(2,1)S(1)}, bf16[2,2,64,128]{3,2,1,0:T(8,128)(2,1)S(1)}, u32[]{:S(2)}, u32[]{:S(2)}) collective-permute-start(bf16[2,2,64,128]{3,2,1,0:T(8,128)(2,1)S(1)} %get-tuple-element.74), channel_id=1, source_target_pairs={{0,8},{8,0},{16,24},{24,16},{1,9},{9,1},{17,25},{25,17},{2,10},{10... | collective-permute-start | bytes 196616 | tf_op jit(solution)/shard_map/ppermute | solution.py:180
